TPU v7x, 512 devices: a whole 4x4x16 slice. The times are simulated.
512 devices in a mesh: head: 4 (over y), tok: 32 (over z, core), hid: 4 (over x).
Axes of the slice: x: 4, y: 4, z: 16, core: 2. Of those that a mesh axis runs over, the one named last changes fastest.
Arguments:
- queries: bfloat16 [16384, 4096], P('tok', 'head'), may hold values from -12 to 12
- keys: bfloat16 [16384, 4096], P('tok', 'head'), may hold values from -12 to 12
- values: bfloat16 [16384, 4096], P('tok', 'head'), may hold values from -12 to 12
- token_rate: float32 [16384, 8], P('tok', 'head'), may hold values from 0.05 to 1
- head_rate: float32 [8], P('head'), may hold values from 0.2 to 1
- w_gate: bfloat16 [8, 512, 1024], P('head', None, 'hid'), may hold values from -0.25 to 0.25
- w_up: bfloat16 [8, 512, 1024], P('head', None, 'hid'), may hold values from -0.25 to 0.25
- w_down: bfloat16 [8, 1024, 512], P('head', 'hid'), may hold values from -0.25 to 0.25
Outputs:
- result: bfloat16 [16384, 4096], P('tok', ('head', 'hid'))
All inputs are finite; a program needn't handle non-finite values.
Results may differ from a plain program's by a relative error of at most 0.035.
Values may be sent and summed in bfloat16 or wider, within the bound.
No kernel may reach another device: no remote copies, remote signals or barrier semaphores. Data moves between devices by JAX's collectives and lax.ppermute only.
A program may use at most 64 MiB of HBM per device.

v0:
```python
import jax
import jax.numpy as jnp
from jax import lax
from jax.sharding import Mesh
from jax.sharding import PartitionSpec as P

NS_ITERS = 3
TOK = ("tok_0", "tok_1")


poly_a = 3.4445
poly_b = -4.775
poly_c = 2.0315


def copy_for_each(shard, axis):
    size = lax.axis_size(axis)
    return lax.all_to_all(
        jnp.broadcast_to(shard[None], (size, *shard.shape)), axis, 0, 0, tiled=True
    )


def in_order(pieces, dim):
    pieces = jnp.moveaxis(pieces, 0, dim)
    dims = pieces.shape
    return pieces.reshape(*dims[:dim], dims[dim] * dims[dim + 1], *dims[dim + 2 :])


def gather_axes(shard, axes, dim):
    far, near = axes
    leading = copy_for_each(shard, far)
    pieces = jnp.swapaxes(copy_for_each(leading, near), 0, 1)
    return in_order(pieces.reshape(-1, *shard.shape), dim)


def cut_along(shard, dim, size):
    before, after = (shard.shape[:dim], shard.shape[dim + 1 :])
    return jnp.moveaxis(shard.reshape(*before, size, -1, *after), dim, 0)


def sum_at_owner(shard, axis, dim):
    size = lax.axis_size(axis)
    pieces = lax.all_to_all(cut_along(shard, dim, size), axis, 0, 0, tiled=True)
    return jnp.sum(pieces.astype(jnp.float32), axis=0)


def sum_in_two_steps(shard, axes, dim):
    far, near = axes
    own = sum_at_owner(cut_along(shard, dim, lax.axis_size(far)), near, dim + 1)
    return jnp.sum(
        lax.all_to_all(own.astype(jnp.bfloat16), far, 0, 0, tiled=True).astype(jnp.float32), axis=0
    )


def over_copies(shard, axis):
    everything = copy_for_each(shard, axis)
    return jnp.sum(everything, axis=0)


def over_axes(shard, axes):
    far, near = axes
    return over_copies(over_copies(shard, near), far)


def over_copies_2(shard, axis):
    everything = copy_for_each(shard, axis)
    return jnp.sum(everything.astype(jnp.float32), axis=0)


def rescale(fresh, previous, which_dim):
    old_norm = jnp.sqrt(
        jnp.sum(jnp.square(previous.astype(jnp.float32)), axis=which_dim, keepdims=True)
    )
    new_norm = jnp.sqrt(jnp.sum(fresh * fresh, axis=which_dim, keepdims=True) + 1e-06)
    return (fresh * old_norm / new_norm).astype(jnp.bfloat16)


def gather_rows(iterate):
    return gather_axes(iterate, ("tok_0", "tok_1"), 1)


def local(queries, keys, values, token_rate, head_rate, w_gate, w_up, w_down):
    tok_rows, all_cols = keys.shape
    heads_here = token_rate.shape[1]
    head_width = all_cols // heads_here
    unit_count = w_gate.shape[2]
    tok_count = lax.axis_size(TOK)
    row_share = head_width // tok_count
    problems = 3 * heads_here
    key_rows = keys.reshape(tok_rows, heads_here, head_width)
    value_rows = values.reshape(tok_rows, heads_here, head_width)
    query_rows = queries.reshape(tok_rows, heads_here, head_width)
    gate_pre = jnp.einsum("thd,hdf->thf", key_rows, w_gate, preferred_element_type=jnp.float32)
    up_pre = jnp.einsum("thd,hdf->thf", key_rows, w_up, preferred_element_type=jnp.float32)
    gate_sig = jax.nn.sigmoid(gate_pre)
    active = gate_pre * gate_sig
    hidden_keys = (active * up_pre).astype(jnp.bfloat16)
    target = (-(token_rate[:, :, None] * value_rows.astype(jnp.float32))).astype(jnp.bfloat16)
    back_hidden = jnp.einsum("thd,hfd->thf", target, w_down, preferred_element_type=jnp.float32)
    grad_gate = (back_hidden * up_pre * gate_sig * (1.0 + gate_pre * (1.0 - gate_sig))).astype(
        jnp.bfloat16
    )
    grad_up = (back_hidden * active).astype(jnp.bfloat16)
    term_gate = jnp.einsum("thc,thf->chf", key_rows, grad_gate, preferred_element_type=jnp.float32)
    term_up = jnp.einsum("thc,thf->chf", key_rows, grad_up, preferred_element_type=jnp.float32)
    term_down = jnp.einsum("thc,thf->chf", target, hidden_keys, preferred_element_type=jnp.float32)
    owned = sum_in_two_steps(
        jnp.stack((term_gate, term_up, term_down), axis=2).astype(jnp.bfloat16),
        ("tok_0", "tok_1"),
        0,
    )
    owned = owned.reshape(row_share, problems, unit_count).transpose(1, 0, 2)
    sq_norm = over_axes(jnp.sum(owned * owned, axis=(1, 2)), (("tok_0", "tok_1"), "hid"))
    current = (owned / (jnp.sqrt(sq_norm)[:, None, None] + 1e-07)).astype(jnp.bfloat16)
    gathered = None
    for iteration in range(NS_ITERS):
        gathered = gather_rows(current)
        gram_part = jnp.einsum(
            "prf,pcf->prc", current, gathered, preferred_element_type=jnp.float32
        )
        gram_rows = (
            over_copies_2(gram_part.astype(jnp.bfloat16), "hid")
            .astype(jnp.float32)
            .astype(jnp.bfloat16)
        )
        product = jnp.einsum(
            "prc,pcf->prf", gram_rows, gathered, preferred_element_type=jnp.float32
        ).astype(jnp.bfloat16)
        second = jnp.einsum(
            "prc,pcf->prf",
            gram_rows,
            gather_axes(product, ("tok_0", "tok_1"), 1),
            preferred_element_type=jnp.float32,
        )
        current = (
            poly_a * current.astype(jnp.float32)
            + poly_b * product.astype(jnp.float32)
            + poly_c * second
        ).astype(jnp.bfloat16)
        gathered = None
    ortho_full = gather_rows(current).reshape(heads_here, 3, head_width, unit_count)
    step_rate = head_rate[:, None, None]
    gate_new = rescale(
        w_gate.astype(jnp.float32) - step_rate * ortho_full[:, 0].astype(jnp.float32), w_gate, 1
    )
    up_new = rescale(
        w_up.astype(jnp.float32) - step_rate * ortho_full[:, 1].astype(jnp.float32), w_up, 1
    )
    down_new = rescale(
        w_down.astype(jnp.float32)
        - step_rate * jnp.swapaxes(ortho_full[:, 2], 1, 2).astype(jnp.float32),
        w_down,
        2,
    )
    query_gate = jnp.einsum(
        "thd,hdf->thf", query_rows, gate_new, preferred_element_type=jnp.float32
    )
    query_up = jnp.einsum("thd,hdf->thf", query_rows, up_new, preferred_element_type=jnp.float32)
    query_hidden = (jax.nn.silu(query_gate) * query_up).astype(jnp.bfloat16)
    partial_value = jnp.einsum(
        "thf,hfd->thd", query_hidden, down_new, preferred_element_type=jnp.float32
    ).reshape(tok_rows, all_cols)
    return sum_at_owner(partial_value.astype(jnp.bfloat16), "hid", 1).astype(jnp.bfloat16)


def solution(mesh):
    finer = Mesh(
        mesh.devices.reshape(mesh.shape["head"], 16, 2, mesh.shape["hid"]),
        ("head", "tok_0", "tok_1", "hid"),
    )
    return jax.shard_map(
        local,
        mesh=finer,
        in_specs=(
            P(TOK, "head"),
            P(TOK, "head"),
            P(TOK, "head"),
            P(TOK, "head"),
            P("head"),
            P("head", None, "hid"),
            P("head", None, "hid"),
            P("head", "hid", None),
        ),
        out_specs=P(TOK, ("head", "hid")),
        check_vma=False,
    )
```

profile of v0, /device:TPU:1, one launch (start us, length us, event | category | flops | bytes accessed | tf_op | source)
XLA Modules:
  0.0 522.8 jit_solution(9150018752788023572)
XLA Ops:
  0.0 1.9 convolution_bitcast_fusion.3
  1.9 0.4 convolution_bitcast_fusion.2
  2.4 0.8 copy-done.5
  3.2 0.2 convert_element_type.177
  3.4 0.8 copy-done.3
  4.2 0.5 convolution_bitcast_fusion.4
  4.7 0.7 fusion.6
  5.4 0.6 fusion.5
  6.0 0.7 fusion.4
  6.7 0.2 copy.245
  6.9 0.2 copy.243
  7.1 0.2 copy.240
  7.3 0.2 maximum_bitcast_fusion
  7.5 0.2 copy.246
  7.6 11.5 %all_to_all.112 = bf16[2,16,16,2,3,256]{5,2,1,3,4,0:T(8,128)(2,1)S(1)} all-to-all(bf16[2,16,16,2,3,256]{5,2,1,3,4,0:T(8,128)(2,1)S(1)} %copy.246), channel_id=1, replica_groups=mesh['head'=4,'tok_0'=16,'tok_1'=2,'hid'=4] {'tok_1'}, dimensions={0} | all-to-all | bytes 3145728 | tf_op jit(solution)/shard_map/all_to_all | solution.py:43
  19.1 0.7 reduce_sum.150
  19.9 45.1 %all_to_all.113 = bf16[16,16,2,3,256]{4,1,3,2,0:T(8,128)(2,1)S(1)} all-to-all(bf16[16,16,2,3,256]{4,1,3,2,0:T(8,128)(2,1)S(1)} %copy.248), channel_id=1, replica_groups=mesh['head'=4,'tok_0'=16,'tok_1'=2,'hid'=4] {'tok_0'}, dimensions={0} | all-to-all | bytes 1572864 | tf_op jit(solution)/shard_map/all_to_all | solution.py:51
  65.3 7.9 %all_to_all.114 = f32[4,1,6]{2,1,0:T(1,128)S(1)} all-to-all(f32[4,1,6]{2,1,0:T(1,128)S(1)} %broadcast_in_dim.38), channel_id=1, replica_groups=mesh['head'=4,'tok_0'=16,'tok_1'=2,'hid'=4] {'hid'}, dimensions={0} | all-to-all | bytes 192 | tf_op jit(solution)/shard_map/all_to_all | solution.py:18
  73.3 24.9 %all_to_all.115 = f32[32,1,6]{2,1,0:T(1,128)S(1)} all-to-all(f32[32,1,6]{2,1,0:T(1,128)S(1)} %broadcast_in_dim.39), channel_id=1, replica_groups=mesh['head'=4,'tok_0'=16,'tok_1'=2,'hid'=4] {'tok_0','tok_1'}, dimensions={0} | all-to-all | bytes 1536 | tf_op jit(solution)/shard_map/all_to_all | solution.py:18
  98.4 38.1 %all_to_all.116 = bf16[16,6,16,256]{3,2,1,0:T(8,128)(2,1)S(1)} all-to-all(bf16[16,6,16,256]{3,2,1,0:T(8,128)(2,1)S(1)} %broadcast_in_dim.40), channel_id=1, replica_groups=mesh['head'=4,'tok_0'=16,'tok_1'=2,'hid'=4] {'tok_0'}, dimensions={0} | all-to-all | bytes 1572864 | tf_op jit(solution)/shard_map/all_to_all | solution.py:18
  136.7 11.2 %all_to_all.117 = bf16[2,16,6,16,256]{4,3,1,2,0:T(8,128)(2,1)S(1)} all-to-all(bf16[2,16,6,16,256]{4,3,1,2,0:T(8,128)(2,1)S(1)} %broadcast_in_dim.41), channel_id=1, replica_groups=mesh['head'=4,'tok_0'=16,'tok_1'=2,'hid'=4] {'tok_1'}, dimensions={0} | all-to-all | bytes 3145728 | tf_op jit(solution)/shard_map/all_to_all | solution.py:18
  147.9 0.2 copy.252
  148.2 0.5 convolution_convert_fusion.6
  148.8 10.2 %all_to_all.118 = bf16[4,6,16,512]{3,2,1,0:T(8,128)(2,1)S(1)} all-to-all(bf16[4,6,16,512]{3,2,1,0:T(8,128)(2,1)S(1)} %broadcast_in_dim.42), channel_id=1, replica_groups=mesh['head'=4,'tok_0'=16,'tok_1'=2,'hid'=4] {'hid'}, dimensions={0} | all-to-all | bytes 786432 | tf_op jit(solution)/shard_map/all_to_all | solution.py:18
  159.1 0.3 convolution_convert_fusion.9
  159.5 40.4 %all_to_all.119 = bf16[16,6,16,256]{3,2,1,0:T(8,128)(2,1)S(1)} all-to-all(bf16[16,6,16,256]{3,2,1,0:T(8,128)(2,1)S(1)} %broadcast_in_dim.43), channel_id=1, replica_groups=mesh['head'=4,'tok_0'=16,'tok_1'=2,'hid'=4] {'tok_0'}, dimensions={0} | all-to-all | bytes 1572864 | tf_op jit(solution)/shard_map/all_to_all | solution.py:18
  200.1 11.5 %all_to_all.120 = bf16[2,16,6,16,256]{4,3,1,2,0:T(8,128)(2,1)S(1)} all-to-all(bf16[2,16,6,16,256]{4,3,1,2,0:T(8,128)(2,1)S(1)} %broadcast_in_dim.44), channel_id=1, replica_groups=mesh['head'=4,'tok_0'=16,'tok_1'=2,'hid'=4] {'tok_1'}, dimensions={0} | all-to-all | bytes 3145728 | tf_op jit(solution)/shard_map/all_to_all | solution.py:18
  211.6 0.2 copy.255
  211.9 0.3 fusion.10
  212.3 40.7 %all_to_all.121 = bf16[16,6,16,256]{3,2,1,0:T(8,128)(2,1)S(1)} all-to-all(bf16[16,6,16,256]{3,2,1,0:T(8,128)(2,1)S(1)} %broadcast_in_dim.45), channel_id=1, replica_groups=mesh['head'=4,'tok_0'=16,'tok_1'=2,'hid'=4] {'tok_0'}, dimensions={0} | all-to-all | bytes 1572864 | tf_op jit(solution)/shard_map/all_to_all | solution.py:18
  253.2 11.1 %all_to_all.122 = bf16[2,16,6,16,256]{4,3,1,2,0:T(8,128)(2,1)S(1)} all-to-all(bf16[2,16,6,16,256]{4,3,1,2,0:T(8,128)(2,1)S(1)} %broadcast_in_dim.46), channel_id=1, replica_groups=mesh['head'=4,'tok_0'=16,'tok_1'=2,'hid'=4] {'tok_1'}, dimensions={0} | all-to-all | bytes 3145728 | tf_op jit(solution)/shard_map/all_to_all | solution.py:18
  264.3 0.2 copy.258
  264.6 0.5 convolution_convert_fusion.5
  265.2 10.2 %all_to_all.123 = bf16[4,6,16,512]{3,2,1,0:T(8,128)(2,1)S(1)} all-to-all(bf16[4,6,16,512]{3,2,1,0:T(8,128)(2,1)S(1)} %broadcast_in_dim.47), channel_id=1, replica_groups=mesh['head'=4,'tok_0'=16,'tok_1'=2,'hid'=4] {'hid'}, dimensions={0} | all-to-all | bytes 786432 | tf_op jit(solution)/shard_map/all_to_all | solution.py:18
  275.4 0.3 convolution_convert_fusion.8
  275.8 40.2 %all_to_all.124 = bf16[16,6,16,256]{3,2,1,0:T(8,128)(2,1)S(1)} all-to-all(bf16[16,6,16,256]{3,2,1,0:T(8,128)(2,1)S(1)} %broadcast_in_dim.48), channel_id=1, replica_groups=mesh['head'=4,'tok_0'=16,'tok_1'=2,'hid'=4] {'tok_0'}, dimensions={0} | all-to-all | bytes 1572864 | tf_op jit(solution)/shard_map/all_to_all | solution.py:18
  316.3 11.5 %all_to_all.125 = bf16[2,16,6,16,256]{4,3,1,2,0:T(8,128)(2,1)S(1)} all-to-all(bf16[2,16,6,16,256]{4,3,1,2,0:T(8,128)(2,1)S(1)} %broadcast_in_dim.49), channel_id=1, replica_groups=mesh['head'=4,'tok_0'=16,'tok_1'=2,'hid'=4] {'tok_1'}, dimensions={0} | all-to-all | bytes 3145728 | tf_op jit(solution)/shard_map/all_to_all | solution.py:18
  327.8 0.2 copy.261
  328.1 0.3 fusion.11
  328.5 40.7 %all_to_all.126 = bf16[16,6,16,256]{3,2,1,0:T(8,128)(2,1)S(1)} all-to-all(bf16[16,6,16,256]{3,2,1,0:T(8,128)(2,1)S(1)} %broadcast_in_dim.50), channel_id=1, replica_groups=mesh['head'=4,'tok_0'=16,'tok_1'=2,'hid'=4] {'tok_0'}, dimensions={0} | all-to-all | bytes 1572864 | tf_op jit(solution)/shard_map/all_to_all | solution.py:18
  369.4 11.1 %all_to_all.127 = bf16[2,16,6,16,256]{4,3,1,2,0:T(8,128)(2,1)S(1)} all-to-all(bf16[2,16,6,16,256]{4,3,1,2,0:T(8,128)(2,1)S(1)} %broadcast_in_dim.51), channel_id=1, replica_groups=mesh['head'=4,'tok_0'=16,'tok_1'=2,'hid'=4] {'tok_1'}, dimensions={0} | all-to-all | bytes 3145728 | tf_op jit(solution)/shard_map/all_to_all | solution.py:18
  380.5 0.2 copy.264
  380.8 0.5 convolution_convert_fusion.4
  381.4 10.2 %all_to_all.128 = bf16[4,6,16,512]{3,2,1,0:T(8,128)(2,1)S(1)} all-to-all(bf16[4,6,16,512]{3,2,1,0:T(8,128)(2,1)S(1)} %broadcast_in_dim.52), channel_id=1, replica_groups=mesh['head'=4,'tok_0'=16,'tok_1'=2,'hid'=4] {'hid'}, dimensions={0} | all-to-all | bytes 786432 | tf_op jit(solution)/shard_map/all_to_all | solution.py:18
  391.7 0.3 convolution_convert_fusion.7
  392.1 40.2 %all_to_all.129 = bf16[16,6,16,256]{3,2,1,0:T(8,128)(2,1)S(1)} all-to-all(bf16[16,6,16,256]{3,2,1,0:T(8,128)(2,1)S(1)} %broadcast_in_dim.53), channel_id=1, replica_groups=mesh['head'=4,'tok_0'=16,'tok_1'=2,'hid'=4] {'tok_0'}, dimensions={0} | all-to-all | bytes 1572864 | tf_op jit(solution)/shard_map/all_to_all | solution.py:18
  432.5 11.5 %all_to_all.130 = bf16[2,16,6,16,256]{4,3,1,2,0:T(8,128)(2,1)S(1)} all-to-all(bf16[2,16,6,16,256]{4,3,1,2,0:T(8,128)(2,1)S(1)} %broadcast_in_dim.54), channel_id=1, replica_groups=mesh['head'=4,'tok_0'=16,'tok_1'=2,'hid'=4] {'tok_1'}, dimensions={0} | all-to-all | bytes 3145728 | tf_op jit(solution)/shard_map/all_to_all | solution.py:18
  444.0 0.2 copy.267
  444.4 0.3 fusion.12
  444.7 1.0 broadcast_in_dim.55
  445.6 5.1 all-to-all-start.19
  450.7 0.2 copy.230
  451.0 34.0 %all-to-all-done.19 = bf16[16,6,16,256]{3,2,1,0:T(8,128)(2,1)S(1)} async-done(((bf16[16,6,16,256]{3,2,1,0:T(8,128)(2,1)}), bf16[16,6,16,256]{3,2,1,0:T(8,128)(2,1)S(1)}, u32[]{:S(2)}, u32[]{:S(2)}) %all-to-all-start.19) | async-done | bytes 786464 | tf_op jit(solution)/shard_map/all_to_all | solution.py:18
  485.0 0.2 broadcast_in_dim.56
  485.2 10.5 %all_to_all.131 = bf16[2,16,6,16,256]{4,3,2,1,0:T(8,128)(2,1)S(1)} all-to-all(bf16[2,16,6,16,256]{4,3,2,1,0:T(8,128)(2,1)S(1)} %broadcast_in_dim.56), channel_id=1, replica_groups=mesh['head'=4,'tok_0'=16,'tok_1'=2,'hid'=4] {'tok_1'}, dimensions={0} | all-to-all | bytes 3145728 | tf_op jit(solution)/shard_map/all_to_all | solution.py:18
  496.0 0.9 copy-done.2
  496.8 0.6 multiply_reduce_fusion
  497.5 0.3 fusion.13
  497.8 0.3 copy-done.8
  498.1 1.6 convolution_bitcast_fusion.1
  499.7 3.7 convolution_convert_fusion
  503.4 18.3 %all_to_all.132 = bf16[4,512,256]{1,2,0:T(8,128)(2,1)S(1)} all-to-all(bf16[4,512,256]{1,2,0:T(8,128)(2,1)} %bitcast.199), channel_id=1, replica_groups=mesh['head'=4,'tok_0'=16,'tok_1'=2,'hid'=4] {'hid'}, dimensions={0} | all-to-all | bytes 2097152 | tf_op jit(solution)/shard_map/all_to_all | solution.py:43
  521.7 0.2 reduce_sum.164
  522.0 0.8 copy.279
  (60 shorter events, 3.7 us)
Async XLA Ops:
  0.0 1.9 copy-start
  0.0 1.9 copy-start.1
  1.9 1.2 copy-start.5
  3.2 1.0 copy-start.3
  3.2 1.0 copy-start.6
  444.7 6.1 %copy-start.4 = (bf16[2,256,512]{2,1,0:T(8,128)(2,1)S(1)}, bf16[2,256,512]{2,1,0:T(8,128)(2,1)}, u32[]{:S(2)}) copy-start(bf16[2,256,512]{2,1,0:T(8,128)(2,1)} %param.15) | copy-start | bytes 1572868
  445.6 39.4 %all-to-all-start.19 = ((bf16[16,6,16,256]{3,2,1,0:T(8,128)(2,1)}), bf16[16,6,16,256]{3,2,1,0:T(8,128)(2,1)S(1)}, u32[]{:S(2)}, u32[]{:S(2)}) async-start(bf16[16,6,16,256]{3,2,1,0:T(8,128)(2,1)} %broadcast_in_dim.55), calls=%async_computation.19 | async-start | bytes 1572864 | tf_op jit(solution)/shard_map/all_to_all | solution.py:18
  495.8 1.0 copy-start.2
  495.8 1.0 copy-start.7
  496.8 1.2 copy-start.8
where the time goes:
time: 524 us; the launch traced here: 523 us
  blocking collectives  457 us (87%)
  waiting for transfers between devices  34 us (6%)
  matrix products  13.6 us (3%)
  local copies, waits for them, and re-layouts  9.93 us (2%)
    all_to_all x18, blocking collectives, copy_for_each(): lax.all_to_all(jnp.broadcast_to(shard[None], (size, *shard.shape)), axis,...  382 us
    all_to_all x1, blocking collectives, sum_in_two_steps(): lax.all_to_all(own.astype(jnp.bfloat16), far, 0, 0, tiled=True)  45.1 us
    all_to_all x1, waiting for transfers between devices, copy_for_each(): lax.all_to_all(jnp.broadcast_to(shard[None], (size, *shard.shape)), axis,...  34 us
    all_to_all x2, blocking collectives, sum_at_owner(): pieces = lax.all_to_all(cut_along(shard, dim, size), axis, 0, 0, tiled=True)  29.8 us
  transfers between devices with their start and end apart: 1, of which 1 were waited for; matrix products, arithmetic and copies ran while one was open for 0% of the time, Pallas kernels for 0%

commit v1 on v0

v1 whole, which is shorter than its diff:
```python
import jax
import jax.numpy as jnp
from jax import lax
from jax.sharding import Mesh
from jax.sharding import PartitionSpec as P

NS_ITERS = 3
FAR = 4
NEAR = 4
TOK = ("far", "near", "core")

poly_a = 3.4445
poly_b = -4.775
poly_c = 2.0315


def dot32(left, right, contract):
    return lax.dot_general(left, right, (contract, ((), ())), preferred_element_type=jnp.float32)


def sum_of_copies(pieces, axis):
    got = lax.all_to_all(pieces, axis, 0, 0, tiled=True)
    return jnp.sum(got.astype(jnp.float32), axis=0)


def copies_from(shard, axis):
    size = lax.axis_size(axis)
    return lax.all_to_all(
        jnp.broadcast_to(shard[None], (size, *shard.shape)), axis, 0, 0, tiled=True
    )


def head_gradients(keys, values, rate, gate, up, down):
    gate_pre = dot32(keys, gate, ((1,), (0,)))
    up_pre = dot32(keys, up, ((1,), (0,)))
    gate_sig = jax.nn.sigmoid(gate_pre)
    active = gate_pre * gate_sig
    hidden_keys = (active * up_pre).astype(jnp.bfloat16)
    target = (-(rate * values.astype(jnp.float32))).astype(jnp.bfloat16)
    back_hidden = dot32(target, down, ((1,), (1,)))
    grad_gate = (back_hidden * up_pre * gate_sig * (1.0 + gate_pre * (1.0 - gate_sig))).astype(
        jnp.bfloat16
    )
    grad_up = (back_hidden * active).astype(jnp.bfloat16)
    return jnp.stack(
        (
            dot32(keys, grad_gate, ((0,), (0,))),
            dot32(keys, grad_up, ((0,), (0,))),
            dot32(target, hidden_keys, ((0,), (0,))),
        )
    )


def newton_schulz(blocks, own):
    sq_norm = jnp.sum(jnp.square(blocks.astype(jnp.float32)))
    scale = 1.0 / (jnp.sqrt(sq_norm) + 1e-07)
    current = blocks
    for iteration in range(NS_ITERS):
        first = scale if iteration == 0 else None
        gram = jnp.einsum("xrf,xcf->rc", current, current, preferred_element_type=jnp.float32)
        if first is not None:
            gram = gram * (first * first)
        gram = gram.astype(jnp.bfloat16)
        if iteration == NS_ITERS - 1:
            current = lax.dynamic_slice_in_dim(current, own, 1, 0)
        product = jnp.einsum("rc,xcf->xrf", gram, current, preferred_element_type=jnp.float32)
        if first is not None:
            product = product * first
        product = product.astype(jnp.bfloat16)
        second = jnp.einsum("rc,xcf->xrf", gram, product, preferred_element_type=jnp.float32)
        leading = current.astype(jnp.float32)
        if first is not None:
            leading = leading * first
        current = (
            poly_a * leading + poly_b * product.astype(jnp.float32) + poly_c * second
        ).astype(jnp.bfloat16)
    return current[0]


def rescale(fresh, previous):
    old_norm = jnp.sqrt(jnp.sum(jnp.square(previous), axis=0, keepdims=True))
    new_norm = jnp.sqrt(jnp.sum(fresh * fresh, axis=0, keepdims=True) + 1e-06)
    return (fresh * old_norm / new_norm).astype(jnp.bfloat16)


def local(queries, keys, values, token_rate, head_rate, w_gate, w_up, w_down):
    tok_rows, all_cols = keys.shape
    heads_here = token_rate.shape[1]
    width = all_cols // heads_here
    units = w_gate.shape[2]
    chunk = width // NEAR
    core = lax.axis_index("core")
    slot = lax.axis_index("far")
    near = lax.axis_index("near")
    hid = lax.axis_index("hid")
    other = 1 - core

    def gradients_of(head):
        cols = head * width
        return head_gradients(
            lax.dynamic_slice_in_dim(keys, cols, width, 1),
            lax.dynamic_slice_in_dim(values, cols, width, 1),
            lax.dynamic_slice_in_dim(token_rate, head, 1, 1),
            lax.dynamic_index_in_dim(w_gate, head, 0, False),
            lax.dynamic_index_in_dim(w_up, head, 0, False),
            lax.dynamic_index_in_dim(w_down, head, 0, False),
        )

    swap = [(0, 1), (1, 0)]
    received = lax.ppermute(gradients_of(other).astype(jnp.bfloat16), "core", swap)
    summed = gradients_of(core) + received.astype(jnp.float32)
    pieces = summed.astype(jnp.bfloat16).reshape(3, NEAR, chunk, units).swapaxes(0, 1)
    near_sum = sum_of_copies(pieces, "near").astype(jnp.bfloat16)
    slots = jnp.concatenate((near_sum, near_sum[:1]), axis=0)
    total = sum_of_copies(slots, "far").astype(jnp.bfloat16)
    rows = lax.all_gather(total, "near", axis=0, tiled=True)
    blocks = copies_from(rows, "hid")
    ortho = newton_schulz(blocks, hid).astype(jnp.float32)

    old = lax.switch(
        jnp.minimum(slot, 2),
        (
            lambda: lax.dynamic_index_in_dim(w_gate, core, 0, False),
            lambda: lax.dynamic_index_in_dim(w_up, core, 0, False),
            lambda: lax.dynamic_index_in_dim(w_down, core, 0, False).T,
        ),
    ).astype(jnp.float32)
    fresh = old - lax.dynamic_index_in_dim(head_rate, core, 0, False) * ortho
    renewed = rescale(fresh, old)
    share = lax.dynamic_slice_in_dim(renewed, near * chunk, chunk, 0)
    by_slot = lax.all_gather(share, "far", axis=0)[:3]
    mine = lax.all_gather(by_slot, "near", axis=1).reshape(3, width, units)
    both = lax.all_gather(mine, "core", axis=0)

    terms = []
    for head in range(heads_here):
        query_rows = queries[:, head * width : (head + 1) * width]
        query_gate = dot32(query_rows, both[head, 0], ((1,), (0,)))
        query_up = dot32(query_rows, both[head, 1], ((1,), (0,)))
        query_hidden = (jax.nn.silu(query_gate) * query_up).astype(jnp.bfloat16)
        term = dot32(query_hidden, both[head, 2], ((1,), (1,))).astype(jnp.bfloat16)
        for half in range(2):
            terms.append(term[:, half * (width // 2) : (half + 1) * (width // 2)])
    return sum_of_copies(jnp.stack(terms), "hid").astype(jnp.bfloat16)


def solution(mesh):
    finer = Mesh(
        mesh.devices.reshape(mesh.shape["head"], FAR, NEAR, 2, mesh.shape["hid"]),
        ("head", "far", "near", "core", "hid"),
    )
    return jax.shard_map(
        local,
        mesh=finer,
        in_specs=(
            P(TOK, "head"),
            P(TOK, "head"),
            P(TOK, "head"),
            P(TOK, "head"),
            P("head"),
            P("head", None, "hid"),
            P("head", None, "hid"),
            P("head", "hid", None),
        ),
        out_specs=P(TOK, ("head", "hid")),
        check_vma=False,
    )
```

time: 524 us -> 207 us (0.40)
  blocking collectives: 457 us -> 110 us
  between operations: 0.51 us -> 14.5 us
  matrix products: 13.6 us -> 23.1 us
  starting transfers between devices: 5.09 us -> 12.9 us
    all_to_all x21 -> x3, blocking collectives: 457 us -> 65.3 us  [sum_of_copies(): got = lax.all_to_all(pieces, axis, 0, 0, tiled=True)]
    all_gather x0 -> x3, blocking collectives: none -> 44.9 us  [the longest x1 19.2 us: local(): by_slot = lax.all_gather(share, 'far', axis=0)[:3]]
    all_gather x0 -> x1, waiting for transfers between devices: none -> 27.3 us  [local(): both = lax.all_gather(mine, 'core', axis=0)]
    all_to_all x1, waiting for transfers between devices: 34 us -> 8.33 us  [copies_from(): lax.all_to_all(jnp.broadcast_to(shard[None], (size, *shard.shape)), axis,...]
    dot_general x17 -> x25, matrix products: 13.6 us -> 23.1 us  [the longest x16 16.5 us: dot32(): lax.dot_general(left, right, (contract, ((), ())), preferred_element_type...]
    ppermute x0 -> x1, starting transfers between devices: none -> 8.91 us  [local(): lax.ppermute(gradients_of(other).astype(jnp.bfloat16), 'core', swap)]
  transfers between devices with their start and end apart: 1 -> 3, of which waited for: 1 -> 2; matrix products, arithmetic and copies ran while one was open for 0% -> 2% of each run, Pallas kernels for 0% -> 0%
where the time goes in v1:
time: 207 us
  blocking collectives  110 us (53%)
  waiting for transfers between devices  35.7 us (17%)
  matrix products  23.1 us (11%)
  between operations  14.5 us (7%)
  starting transfers between devices  12.9 us (6%)
  local copies, waits for them, and re-layouts  6.22 us (3%)
  other arithmetic  3.98 us (2%)
    all_to_all x3, blocking collectives, sum_of_copies(): got = lax.all_to_all(pieces, axis, 0, 0, tiled=True)  65.3 us
    all_gather x1, waiting for transfers between devices, local(): both = lax.all_gather(mine, 'core', axis=0)  27.3 us
    all_gather x1, blocking collectives, local(): by_slot = lax.all_gather(share, 'far', axis=0)[:3]  19.2 us
    dot_general x16, matrix products, dot32(): lax.dot_general(left, right, (contract, ((), ())), preferred_element_type...  16.5 us
    all_gather x1, blocking collectives, local(): mine = lax.all_gather(by_slot, 'near', axis=1).reshape(3, width, units)  14.5 us
    all_gather x1, blocking collectives, local(): rows = lax.all_gather(total, 'near', axis=0, tiled=True)  11.2 us
    ppermute x1, starting transfers between devices, local(): lax.ppermute(gradients_of(other).astype(jnp.bfloat16), 'core', swap)  8.91 us
    all_to_all x1, waiting for transfers between devices, copies_from(): lax.all_to_all(jnp.broadcast_to(shard[None], (size, *shard.shape)), axis,...  8.33 us
  transfers between devices with their start and end apart: 3, of which 2 were waited for; matrix products, arithmetic and copies ran while one was open for 2% of the time, Pallas kernels for 0%

profile of v1, /device:TPU:1, one launch (start us, length us, event | category | flops | bytes accessed | tf_op | source)
XLA Modules:
  0.0 206.5 jit_solution(120781004835603764)
XLA Ops:
  6.5 0.0 copy-start
  6.5 1.2 copy-done
  7.8 1.2 fusion.50
  9.0 1.3 fusion.52
  10.3 0.0 copy-done.6
  10.3 0.0 copy-done.5
  10.3 1.4 fusion.64
  11.7 0.4 fusion.27
  12.2 0.0 copy-start.7
  12.2 0.5 fusion.26
  12.7 0.7 copy-done.7
  13.4 0.6 fusion.28
  14.0 0.0 copy-start.2
  14.0 0.1 pad_maximum_fusion.1
  14.1 0.0 copy-start.1
  14.1 8.9 %collective-permute-start = (bf16[3,512,256]{2,1,0:T(8,128)(2,1)S(1)}, bf16[3,512,256]{2,1,0:T(8,128)(2,1)}, u32[]{:S(2)}, u32[]{:S(2)}) collective-permute-start(bf16[3,512,256]{2,1,0:T(8,128)(2,1)S(1)} %pad_maximum_fusion.1), channel_id=1, source_target_pairs={{0,4},{4,0},{1,5},{5,1},{2,6},{6,2},{3,7},{7,3},{8,12},{12,8},{9,1... | collective-permute-start | bytes 2359304 | tf_op jit(solution)/shard_map/ppermute | solution.py:110
  23.0 0.0 copy-done.2
  23.0 0.3 fusion.56
  23.3 1.5 fusion.68
  24.8 0.3 fusion.58
  25.1 0.0 copy-start.8
  25.1 0.4 convolution_bitcast_fusion.8
  25.6 0.8 copy-done.8
  26.4 0.5 convolution_bitcast_fusion.7
  26.9 0.5 convolution_bitcast_fusion.9
  27.4 0.0 collective-permute-done
  27.4 1.4 fusion.6
  28.8 0.1 copy.73
  28.9 22.4 %all_to_all.20 = bf16[4,3,128,256]{3,2,1,0:T(8,128)(2,1)S(1)} all-to-all(bf16[4,3,128,256]{3,2,1,0:T(8,128)(2,1)S(1)} %bitcast.176), channel_id=1, replica_groups=mesh['head'=4,'far'=4,'near'=4,'core'=2,'hid'=4] {'near'}, dimensions={0} | all-to-all | bytes 1572864 | tf_op jit(solution)/shard_map/all_to_all | solution.py:22
  51.2 0.2 reduce_sum.63
  51.4 25.4 %all_to_all.21 = bf16[4,128,256]{2,1,0:T(8,128)(2,1)S(1)} all-to-all(bf16[4,128,256]{2,1,0:T(8,128)(2,1)S(1)} %pad_maximum_fusion.2), channel_id=1, replica_groups=mesh['head'=4,'far'=4,'near'=4,'core'=2,'hid'=4] {'far'}, dimensions={0} | all-to-all | bytes 524288 | tf_op jit(solution)/shard_map/all_to_all | solution.py:22
  76.9 11.2 %all_gather.18 = bf16[512,256]{1,0:T(8,128)(2,1)S(1)} all-gather(bf16[128,256]{1,0:T(8,128)(2,1)S(1)} %reduce_sum.64), channel_id=1, replica_groups=mesh['head'=4,'far'=4,'near'=4,'core'=2,'hid'=4] {'near'}, dimensions={0}, use_global_device_ids=true | all-gather | bytes 327680 | tf_op jit(solution)/shard_map/all_gather | solution.py:116
  88.1 1.0 broadcast_in_dim.2
  89.2 4.0 %all-to-all-start.2 = ((bf16[4,512,256]{2,1,0:T(8,128)(2,1)}), bf16[4,512,256]{2,1,0:T(8,128)(2,1)S(1)}, u32[]{:S(2)}, u32[]{:S(2)}) async-start(bf16[4,512,256]{2,1,0:T(8,128)(2,1)} %broadcast_in_dim.2), calls=%async_computation.2 | async-start | bytes 2097152 | tf_op jit(solution)/shard_map/all_to_all | solution.py:28
  93.2 0.2 conditional.1
  93.2 0.2 copy.40
  93.5 0.1 copy.42
  93.6 0.3 copy-done.9
  93.9 0.6 dynamic_slice.57
  94.5 0.1 fusion.29
  94.6 8.3 %all-to-all-done.2 = bf16[4,512,256]{2,1,0:T(8,128)(2,1)S(1)} async-done(((bf16[4,512,256]{2,1,0:T(8,128)(2,1)}), bf16[4,512,256]{2,1,0:T(8,128)(2,1)S(1)}, u32[]{:S(2)}, u32[]{:S(2)}) %all-to-all-start.2) | async-done | bytes 1048608 | tf_op jit(solution)/shard_map/all_to_all | solution.py:28
  102.9 1.1 fusion
  104.8 0.7 fusion.14
  105.5 0.7 fusion.7
  106.3 0.8 fusion.4
  107.1 0.7 fusion.13
  107.9 0.7 fusion.9
  108.6 0.8 fusion.5
  109.4 0.7 fusion.12
  110.1 0.3 convolution_convert_fusion.3
  110.4 1.0 multiply_reduce_fusion
  111.5 19.2 %all-gather = bf16[512,256]{1,0:T(8,128)(2,1)S(1)} all-gather(bf16[128,256]{1,0:T(8,128)(2,1)S(1)} %fusion.81), channel_id=2, replica_groups=mesh['head'=4,'far'=4,'near'=4,'core'=2,'hid'=4] {'far'}, dimensions={0}, use_global_device_ids=true | all-gather | bytes 327680 | tf_op jit(solution)/shard_map/all_gather | solution.py:131
  130.7 14.5 %all-gather.1 = bf16[3,512,256]{2,1,0:T(8,128)(2,1)} all-gather(bf16[3,128,256]{2,1,0:T(8,128)(2,1)S(1)} %bitcast.178), channel_id=3, replica_groups=mesh['head'=4,'far'=4,'near'=4,'core'=2,'hid'=4] {'near'}, dimensions={1}, use_global_device_ids=true | all-gather | bytes 983040 | tf_op jit(solution)/shard_map/all_gather | solution.py:132
  145.2 0.0 all-gather.5.cloned.1.call-update
  145.2 27.3 %all-gather.5.cloned.1.call-done = bf16[6,512,256]{2,1,0:T(8,128)(2,1)} async-done(((bf16[3,512,256]{2,1,0:T(8,128)(2,1)}), bf16[6,512,256]{2,1,0:T(8,128)(2,1)}) %all-gather.5.cloned.1.call-update) | async-done | bytes 1572880 | tf_op jit(solution)/shard_map/all_gather | solution.py:133
  172.5 0.0 copy-done.3
  172.5 1.2 convolution_bitcast_fusion.6
  173.8 1.2 convolution_bitcast_fusion.4
  175.0 2.5 %convolution_convert_fusion.2 = bf16[512,512]{1,0:T(8,128)(2,1)} fusion(f32[512,256]{1,0:T(8,128)S(1)} %convolution_bitcast_fusion.6, bf16[512,1024]{1,0:T(8,128)(2,1)S(1)} %copy-done.3, bf16[2,3,512,256]{3,2,1,0:T(8,128)(2,1)} %bitcast.181), kind=kOutput, calls=%fused_computation.26 | convolution fusion | flops 269484032 | bytes 2097152 | tf_op jit(solution)/shard_map/dot_general | solution.py:18
  177.5 2.6 %convolution_convert_fusion.1 = bf16[512,512]{1,0:T(8,128)(2,1)} fusion(f32[512,256]{1,0:T(8,128)S(1)} %convolution_bitcast_fusion.4, bf16[512,1024]{1,0:T(8,128)(2,1)S(1)} %copy-done.3, bf16[2,3,512,256]{3,2,1,0:T(8,128)(2,1)} %bitcast.182), kind=kOutput, calls=%fused_computation.25 | convolution fusion | flops 269484032 | bytes 2097152 | tf_op jit(solution)/shard_map/dot_general | solution.py:18
  180.1 1.1 slice_bitcast_fusion.1
  181.2 0.1 pad_maximum_fusion
  181.3 17.5 %all_to_all.22 = bf16[4,512,256]{2,1,0:T(8,128)(2,1)S(1)} all-to-all(bf16[4,512,256]{2,1,0:T(8,128)(2,1)S(1)} %pad_maximum_fusion), channel_id=1, replica_groups=mesh['head'=4,'far'=4,'near'=4,'core'=2,'hid'=4] {'hid'}, dimensions={0} | all-to-all | bytes 2097152 | tf_op jit(solution)/shard_map/all_to_all | solution.py:22
  198.8 0.9 reduce_sum.68
  (17 shorter events, 0.2 us)
Async XLA Ops:
  6.5 1.2 copy-start
  6.5 3.7 %copy-start.6 = (f32[512,2]{0,1:T(2,128)S(1)}, f32[512,2]{0,1:T(2,128)}, u32[]{:S(2)}) copy-start(f32[512,2]{0,1:T(2,128)} %param.14) | copy-start | bytes 12292
  6.5 3.8 %copy-start.5 = (bf16[2,256,512]{2,1,0:T(8,128)(2,1)S(1)}, bf16[2,256,512]{2,1,0:T(8,128)(2,1)}, u32[]{:S(2)}) copy-start(bf16[2,256,512]{2,1,0:T(8,128)(2,1)} %param.18) | copy-start | bytes 1572868
  12.2 1.2 copy-start.7
  14.0 9.0 %copy-start.2 = (bf16[2,512,256]{2,1,0:T(8,128)(2,1)S(1)}, bf16[2,512,256]{2,1,0:T(8,128)(2,1)}, u32[]{:S(2)}) copy-start(bf16[2,512,256]{2,1,0:T(8,128)(2,1)} %param.16) | copy-start | bytes 1572868
  14.1 10.7 %copy-start.1 = (bf16[2,512,256]{2,1,0:T(8,128)(2,1)S(1)}, bf16[2,512,256]{2,1,0:T(8,128)(2,1)}, u32[]{:S(2)}) copy-start(bf16[2,512,256]{2,1,0:T(8,128)(2,1)} %param.17) | copy-start | bytes 1572868
  14.1 13.3 %collective-permute-start = (bf16[3,512,256]{2,1,0:T(8,128)(2,1)S(1)}, bf16[3,512,256]{2,1,0:T(8,128)(2,1)}, u32[]{:S(2)}, u32[]{:S(2)}) collective-permute-start(bf16[3,512,256]{2,1,0:T(8,128)(2,1)S(1)} %pad_maximum_fusion.1), channel_id=1, source_target_pairs={{0,4},{4,0},{1,5},{5,1},{2,6},{6,2},{3,7},{7,3},{8,12},{12,8},{9,1... | collective-permute-start | bytes 2359304 | tf_op jit(solution)/shard_map/ppermute | solution.py:110
  25.1 1.2 copy-start.8
  89.2 13.8 %all-to-all-start.2 = ((bf16[4,512,256]{2,1,0:T(8,128)(2,1)}), bf16[4,512,256]{2,1,0:T(8,128)(2,1)S(1)}, u32[]{:S(2)}, u32[]{:S(2)}) async-start(bf16[4,512,256]{2,1,0:T(8,128)(2,1)} %broadcast_in_dim.2), calls=%async_computation.2 | async-start | bytes 2097152 | tf_op jit(solution)/shard_map/all_to_all | solution.py:28
  93.2 79.3 %all-gather.5.cloned.1.call-start = ((), (), s32[]{:S(2)}) async-start(), calls=%async_computation.4 | async-start | bytes 2359296 | tf_op jit(solution)/shard_map/all_gather | solution.py:133
  93.2 0.7 copy-start.9
  111.4 61.1 %copy-start.3 = (bf16[512,1024]{1,0:T(8,128)(2,1)S(1)}, bf16[512,1024]{1,0:T(8,128)(2,1)}, u32[]{:S(2)}) copy-start(bf16[512,1024]{1,0:T(8,128)(2,1)} %param.11) | copy-start | bytes 3145732
  177.5 2.6 %copy-start.4 = (bf16[512,512]{1,0:T(8,128)(2,1)S(1)}, bf16[512,512]{1,0:T(8,128)(2,1)}, u32[]{:S(2)}) copy-start(bf16[512,512]{1,0:T(8,128)(2,1)} %convolution_convert_fusion.2) | copy-start | bytes 1572868
Sparse Core Ops, SparseCore 0:
  145.3 27.1 all-gather.4

commit v2 on v1

v2 whole, which is shorter than its diff:
```python
import jax
import jax.numpy as jnp
from jax import lax
from jax.sharding import Mesh
from jax.sharding import PartitionSpec as P

NS_ITERS = 3
TOK = ("z", "core")

poly_a = 3.4445
poly_b = -4.775
poly_c = 2.0315


def dot32(left, right, contract):
    return lax.dot_general(left, right, (contract, ((), ())), preferred_element_type=jnp.float32)


def sum_of_copies(pieces, axis):
    got = lax.all_to_all(pieces, axis, 0, 0, tiled=True)
    return jnp.sum(got.astype(jnp.float32), axis=0)


def head_gradients(keys, values, rate, gate, up, down):
    gate_pre = dot32(keys, gate, ((1,), (0,)))
    up_pre = dot32(keys, up, ((1,), (0,)))
    gate_sig = jax.nn.sigmoid(gate_pre)
    active = gate_pre * gate_sig
    hidden_keys = (active * up_pre).astype(jnp.bfloat16)
    target = (-(rate * values.astype(jnp.float32))).astype(jnp.bfloat16)
    back_hidden = dot32(target, down, ((1,), (1,)))
    grad_gate = (back_hidden * up_pre * gate_sig * (1.0 + gate_pre * (1.0 - gate_sig))).astype(
        jnp.bfloat16
    )
    grad_up = (back_hidden * active).astype(jnp.bfloat16)
    return jnp.stack(
        (
            dot32(keys, grad_gate, ((0,), (0,))),
            dot32(keys, grad_up, ((0,), (0,))),
            dot32(target, hidden_keys, ((0,), (0,))),
        )
    )


def newton_schulz(blocks):
    sq_norm = jnp.sum(jnp.square(blocks.astype(jnp.float32)))
    scale = 1.0 / (jnp.sqrt(sq_norm) + 1e-07)
    current = blocks
    for iteration in range(NS_ITERS):
        factor = scale if iteration == 0 else 1.0
        gram = jnp.einsum("xrf,xcf->rc", current, current, preferred_element_type=jnp.float32)
        gram = (gram * (factor * factor)).astype(jnp.bfloat16)
        product = jnp.einsum("rc,xcf->xrf", gram, current, preferred_element_type=jnp.float32)
        product = (product * factor).astype(jnp.bfloat16)
        second = jnp.einsum("rc,xcf->xrf", gram, product, preferred_element_type=jnp.float32)
        current = (
            poly_a * (factor * current.astype(jnp.float32))
            + poly_b * product.astype(jnp.float32)
            + poly_c * second
        ).astype(jnp.bfloat16)
    return current


def rescale(fresh, previous):
    old_norm = jnp.sqrt(jnp.sum(jnp.square(previous), axis=1, keepdims=True))
    new_norm = jnp.sqrt(jnp.sum(fresh * fresh, axis=1, keepdims=True) + 1e-06)
    return (fresh * old_norm / new_norm).astype(jnp.bfloat16)


def local(queries, keys, values, token_rate, head_rate, w_gate, w_up, w_down):
    tok_rows, all_cols = keys.shape
    width = all_cols // token_rate.shape[1]
    units = w_gate.shape[2]
    chunk = width // lax.axis_size("z")
    core = lax.axis_index("core")
    other = 1 - core

    def gradients_of(head):
        cols = head * width
        return head_gradients(
            lax.dynamic_slice_in_dim(keys, cols, width, 1),
            lax.dynamic_slice_in_dim(values, cols, width, 1),
            lax.dynamic_slice_in_dim(token_rate, head, 1, 1),
            lax.dynamic_index_in_dim(w_gate, head, 0, False),
            lax.dynamic_index_in_dim(w_up, head, 0, False),
            lax.dynamic_index_in_dim(w_down, head, 0, False),
        )

    swap = [(0, 1), (1, 0)]
    received = lax.ppermute(gradients_of(other).astype(jnp.bfloat16), "core", swap)
    summed = gradients_of(core) + received.astype(jnp.float32)
    pieces = summed.astype(jnp.bfloat16).reshape(3, -1, chunk, units).swapaxes(0, 1)
    owned = sum_of_copies(pieces, "z").astype(jnp.bfloat16)
    full = lax.all_gather(owned, "z", axis=1, tiled=True)
    blocks = lax.all_to_all(jnp.concatenate((full, full[:1]), axis=0), "hid", 0, 0, tiled=True)
    ortho = lax.all_to_all(newton_schulz(blocks), "hid", 0, 0, tiled=True)[:3]

    old = jnp.stack(
        (
            lax.dynamic_index_in_dim(w_gate, core, 0, False),
            lax.dynamic_index_in_dim(w_up, core, 0, False),
            lax.dynamic_index_in_dim(w_down, core, 0, False).T,
        )
    ).astype(jnp.float32)
    step = lax.dynamic_index_in_dim(head_rate, core, 0, False)
    mine = rescale(old - step * ortho.astype(jnp.float32), old)
    theirs = lax.ppermute(mine, "core", swap)

    def term_of(head, weights):
        rows = lax.dynamic_slice_in_dim(queries, head * width, width, 1)
        query_gate = dot32(rows, weights[0], ((1,), (0,)))
        query_up = dot32(rows, weights[1], ((1,), (0,)))
        query_hidden = (jax.nn.silu(query_gate) * query_up).astype(jnp.bfloat16)
        halves = [
            dot32(query_hidden, weights[2][part], ((1,), (1,))).astype(jnp.bfloat16)
            for part in (slice(0, width // 2), slice(width // 2, width))
        ]
        return jnp.stack(halves)

    own_term = term_of(core, mine)
    other_term = term_of(other, theirs)
    is_first = core == 0
    terms = jnp.concatenate(
        (
            jnp.where(is_first, own_term, other_term),
            jnp.where(is_first, other_term, own_term),
        )
    )
    return sum_of_copies(terms, "hid").astype(jnp.bfloat16)


def solution(mesh):
    finer = Mesh(
        mesh.devices.reshape(mesh.shape["head"], -1, 2, mesh.shape["hid"]),
        ("head", "z", "core", "hid"),
    )
    return jax.shard_map(
        local,
        mesh=finer,
        in_specs=(
            P(TOK, "head"),
            P(TOK, "head"),
            P(TOK, "head"),
            P(TOK, "head"),
            P("head"),
            P("head", None, "hid"),
            P("head", None, "hid"),
            P("head", "hid", None),
        ),
        out_specs=P(TOK, ("head", "hid")),
        check_vma=False,
    )
```

time: 207 us -> 175 us (0.85)
  waiting for transfers between devices: 35.7 us -> 8.79 us
  between operations: 14.5 us -> 1.15 us
  starting transfers between devices: 12.9 us -> 26.1 us
  blocking collectives: 110 us -> 107 us
  matrix products: 23.1 us -> 20.8 us
    all_gather x1 -> x0, waiting for transfers between devices: 27.3 us -> none  [local(): both = lax.all_gather(mine, 'core', axis=0)]
    all_gather x3 -> x1, blocking collectives: 44.9 us -> 30 us  [local(): full = lax.all_gather(owned, 'z', axis=1, tiled=True)]
    all_to_all x0 -> x1, blocking collectives: none -> 13.6 us  [local(): lax.all_to_all(jnp.concatenate((full, full[:1]), axis=0), 'hid', 0, 0, ti...]
    ppermute x0 -> x1, starting transfers between devices: none -> 13.4 us  [local(): theirs = lax.ppermute(mine, 'core', swap)]
    dot_general x16 -> x20, matrix products: 16.5 us -> 13.1 us  [dot32(): lax.dot_general(left, right, (contract, ((), ())), preferred_element_type...]
    all_to_all x3 -> x2, blocking collectives: 65.3 us -> 63.9 us  [sum_of_copies(): got = lax.all_to_all(pieces, axis, 0, 0, tiled=True)]
  transfers between devices with their start and end apart: 3 -> 3, of which waited for: 2 -> 1; matrix products, arithmetic and copies ran while one was open for 2% -> 5% of each run, Pallas kernels for 0% -> 0%
where the time goes in v2:
time: 175 us
  blocking collectives  107 us (61%)
  starting transfers between devices  26.1 us (15%)
  matrix products  20.8 us (12%)
  waiting for transfers between devices  8.79 us (5%)
  other arithmetic  5.73 us (3%)
  local copies, waits for them, and re-layouts  4.77 us (3%)
    all_to_all x2, blocking collectives, sum_of_copies(): got = lax.all_to_all(pieces, axis, 0, 0, tiled=True)  63.9 us
    all_gather x1, blocking collectives, local(): full = lax.all_gather(owned, 'z', axis=1, tiled=True)  30 us
    all_to_all x1, blocking collectives, local(): lax.all_to_all(jnp.concatenate((full, full[:1]), axis=0), 'hid', 0, 0, ti...  13.6 us
    ppermute x1, starting transfers between devices, local(): theirs = lax.ppermute(mine, 'core', swap)  13.4 us
    dot_general x20, matrix products, dot32(): lax.dot_general(left, right, (contract, ((), ())), preferred_element_type...  13.1 us
    ppermute x1, starting transfers between devices, local(): lax.ppermute(gradients_of(other).astype(jnp.bfloat16), 'core', swap)  8.9 us
    all_to_all x1, waiting for transfers between devices, local(): ortho = lax.all_to_all(newton_schulz(blocks), 'hid', 0, 0, tiled=True)[:3]  8.79 us
    all_to_all x1, starting transfers between devices, local(): ortho = lax.all_to_all(newton_schulz(blocks), 'hid', 0, 0, tiled=True)[:3]  3.83 us
  transfers between devices with their start and end apart: 3, of which 1 were waited for; matrix products, arithmetic and copies ran while one was open for 5% of the time, Pallas kernels for 0%

profile of v2, /device:TPU:1, one launch (start us, length us, event | category | flops | bytes accessed | tf_op | source)
XLA Modules:
  0.0 174.7 jit_solution(17866327132364282736)
XLA Ops:
  0.0 0.0 copy-start
  0.0 1.2 copy-done
  1.2 1.3 fusion.40
  2.5 0.0 copy-done.2
  2.6 0.3 fusion.42
  2.9 0.0 copy-done.5
  2.9 0.0 copy-done.3
  2.9 1.4 fusion.54
  4.3 0.4 fusion.21
  4.8 0.0 copy-start.6
  4.8 0.5 fusion.20
  5.3 0.7 copy-done.6
  6.0 0.6 fusion.22
  6.6 0.0 copy-start.4
  6.6 0.1 pad_maximum_fusion.3
  6.7 8.9 %collective-permute-start = (bf16[3,512,256]{2,1,0:T(8,128)(2,1)S(1)}, bf16[3,512,256]{2,1,0:T(8,128)(2,1)S(1)}, u32[]{:S(2)}, u32[]{:S(2)}) collective-permute-start(bf16[3,512,256]{2,1,0:T(8,128)(2,1)S(1)} %pad_maximum_fusion.3), channel_id=1, source_target_pairs={{0,4},{4,0},{1,5},{5,1},{2,6},{6,2},{3,7},{7,3},{8,12},{12,8},{9,1... | collective-permute-start | bytes 2359304 | tf_op jit(solution)/shard_map/ppermute | solution.py:90
  15.6 1.1 constant_dynamic-slice_fusion.3
  16.7 0.0 copy-start.7
  16.7 0.3 fusion.46
  17.0 0.9 copy-done.7
  17.9 0.3 fusion.50
  18.3 0.4 convolution_bitcast_fusion.4
  18.7 0.3 fusion.48
  19.1 0.5 convolution_bitcast_fusion.3
  19.6 0.5 convolution_bitcast_fusion.5
  20.1 0.0 collective-permute-done
  20.1 0.2 fusion.8
  20.4 0.1 copy.49
  20.4 46.5 %all_to_all.20 = bf16[16,3,32,256]{3,2,1,0:T(8,128)(2,1)S(1)} all-to-all(bf16[16,3,32,256]{3,2,1,0:T(8,128)(2,1)S(1)} %bitcast.138), channel_id=1, replica_groups=mesh['head'=4,'z'=16,'core'=2,'hid'=4] {'z'}, dimensions={0} | all-to-all | bytes 1572864 | tf_op jit(solution)/shard_map/all_to_all | solution.py:20
  67.0 0.1 reduce_sum.51
  67.1 30.0 %all_gather.3 = bf16[3,512,256]{2,1,0:T(8,128)(2,1)S(1)} all-gather(bf16[3,32,256]{2,1,0:T(8,128)(2,1)S(1)} %reduce_sum.51), channel_id=1, replica_groups=mesh['head'=4,'z'=16,'core'=2,'hid'=4] {'z'}, dimensions={1}, use_global_device_ids=true | all-gather | bytes 835584 | tf_op jit(solution)/shard_map/all_gather | solution.py:94
  97.1 0.1 pad_maximum_fusion
  97.2 13.6 %all_to_all.21 = bf16[4,512,256]{2,1,0:T(8,128)(2,1)S(1)} all-to-all(bf16[4,512,256]{2,1,0:T(8,128)(2,1)S(1)} %pad_maximum_fusion), channel_id=1, replica_groups=mesh['head'=4,'z'=16,'core'=2,'hid'=4] {'hid'}, dimensions={0} | all-to-all | bytes 2097152 | tf_op jit(solution)/shard_map/all_to_all | solution.py:95
  110.7 1.1 fusion
  112.6 0.7 fusion.18
  113.4 0.7 fusion.9
  114.1 0.8 fusion.4
  114.9 0.7 fusion.17
  115.7 0.7 fusion.11
  116.4 0.8 fusion.6
  117.2 0.7 fusion.16
  117.9 0.7 fusion.12
  118.7 1.8 %fusion.5 = bf16[4,512,256]{2,1,0:T(8,128)(2,1)} fusion(bf16[4,512,256]{2,1,0:T(8,128)(2,1)S(1)} %fusion.12, bf16[4,512,256]{2,1,0:T(8,128)(2,1)S(1)} %fusion.6, bf16[512,512,1]{1,0,2:T(8,128)(2,1)S(1)} %fusion.16), kind=kOutput, calls=%fused_computation.8 | convolution fusion | flops 541065216 | bytes 3670016 | tf_op jit(solution)/shard_map/rc,xcf->xrf/dot_general | solution.py:55
  120.4 3.8 %all-to-all-start.2 = ((bf16[4,512,256]{2,1,0:T(8,128)(2,1)}), bf16[4,512,256]{2,1,0:T(8,128)(2,1)S(1)}, u32[]{:S(2)}, u32[]{:S(2)}) async-start(bf16[4,512,256]{2,1,0:T(8,128)(2,1)} %fusion.5), calls=%async_computation.2 | async-start | bytes 2097152 | tf_op jit(solution)/shard_map/all_to_all | solution.py:96
  124.3 0.1 copy.22
  124.4 0.6 dynamic_slice.55
  125.0 8.8 %all-to-all-done.2 = bf16[4,512,256]{2,1,0:T(8,128)(2,1)S(1)} async-done(((bf16[4,512,256]{2,1,0:T(8,128)(2,1)}), bf16[4,512,256]{2,1,0:T(8,128)(2,1)S(1)}, u32[]{:S(2)}, u32[]{:S(2)}) %all-to-all-start.2) | async-done | bytes 1048608 | tf_op jit(solution)/shard_map/all_to_all | solution.py:96
  133.8 1.1 fusion.7
  134.9 1.9 %divide_convert_fusion = bf16[3,512,256]{2,1,0:T(8,128)(2,1)} fusion(f32[3,256]{1,0:T(4,128)S(1)} %add_sqrt_fusion, f32[3,256]{1,0:T(4,128)S(1)} %sqrt.20, f32[]{:T(128)} %bitcast.3, bf16[4,512,256]{2,1,0:T(8,128)(2,1)S(1)} %all-to-all-done.2, bf16[1,512,256]{2,1,0:T(8,128)(2,1)S(1)} %bitcast.141, bf16[1,512,256]{2,1,0:T(8,128)(2,1)S(1)} %get-tuple-element.11, ...), kind=kLoop, calls=%fused_computation.17 | loop fusion | flops 3538944 | bytes 2365444 | tf_op jit(solution)/shard_map/convert_element_type | solution.py:67
  136.8 13.4 %collective-permute-start.1 = (bf16[3,512,256]{2,1,0:T(8,128)(2,1)}, bf16[3,512,256]{2,1,0:T(8,128)(2,1)S(1)}, u32[]{:S(2)}, u32[]{:S(2)}) collective-permute-start(bf16[3,512,256]{2,1,0:T(8,128)(2,1)} %divide_convert_fusion), channel_id=1, source_target_pairs={{0,4},{4,0},{1,5},{5,1},{2,6},{6,2},{3,7},{7,3},{8,12},{12,8},{9,1... | collective-permute-start | bytes 2359304 | tf_op jit(solution)/shard_map/ppermute | solution.py:107
  150.1 1.4 fusion.36
  151.6 0.0 copy-done.1
  151.6 1.3 fusion.19
  152.8 1.2 fusion.23
  154.0 1.2 fusion.24
  155.2 0.0 collective-permute-done.1
  155.2 0.3 fusion.31
  155.5 0.3 multiply_convert_fusion.1
  155.8 0.3 fusion.25
  156.1 0.3 fusion.26
  156.3 0.1 broadcast_select_fusion.1
  156.4 0.1 pad_maximum_fusion.1
  156.5 17.3 %all_to_all.22 = bf16[4,512,256]{2,1,0:T(8,128)(2,1)S(1)} all-to-all(bf16[4,512,256]{2,1,0:T(8,128)(2,1)S(1)} %pad_maximum_fusion.1), channel_id=1, replica_groups=mesh['head'=4,'z'=16,'core'=2,'hid'=4] {'hid'}, dimensions={0} | all-to-all | bytes 2097152 | tf_op jit(solution)/shard_map/all_to_all | solution.py:20
  173.8 0.9 reduce_sum.55
  (12 shorter events, 0.1 us)
Async XLA Ops:
  0.0 1.2 copy-start
  0.0 2.5 %copy-start.2 = (bf16[2,512,256]{2,1,0:T(8,128)(2,1)S(1)}, bf16[2,512,256]{2,1,0:T(8,128)(2,1)}, u32[]{:S(2)}) copy-start(bf16[2,512,256]{2,1,0:T(8,128)(2,1)} %param.14) | copy-start | bytes 1572868
  1.2 1.6 copy-start.5
  1.2 1.7 copy-start.3
  4.8 1.2 copy-start.6
  6.6 9.0 %copy-start.4 = (bf16[2,256,512]{2,1,0:T(8,128)(2,1)S(1)}, bf16[2,256,512]{2,1,0:T(8,128)(2,1)}, u32[]{:S(2)}) copy-start(bf16[2,256,512]{2,1,0:T(8,128)(2,1)} %param.15) | copy-start | bytes 1572868
  6.7 13.5 %collective-permute-start = (bf16[3,512,256]{2,1,0:T(8,128)(2,1)S(1)}, bf16[3,512,256]{2,1,0:T(8,128)(2,1)S(1)}, u32[]{:S(2)}, u32[]{:S(2)}) collective-permute-start(bf16[3,512,256]{2,1,0:T(8,128)(2,1)S(1)} %pad_maximum_fusion.3), channel_id=1, source_target_pairs={{0,4},{4,0},{1,5},{5,1},{2,6},{6,2},{3,7},{7,3},{8,12},{12,8},{9,1... | collective-permute-start | bytes 2359304 | tf_op jit(solution)/shard_map/ppermute | solution.py:90
  16.7 1.2 copy-start.7
  120.4 4.0 %copy-start.8 = (f32[2]{0:T(128)S(1)}, f32[2]{0:T(128)}, u32[]{:S(2)}) copy-start(f32[2]{0:T(128)} %param.12) | copy-start | bytes 28
  120.4 13.4 %all-to-all-start.2 = ((bf16[4,512,256]{2,1,0:T(8,128)(2,1)}), bf16[4,512,256]{2,1,0:T(8,128)(2,1)S(1)}, u32[]{:S(2)}, u32[]{:S(2)}) async-start(bf16[4,512,256]{2,1,0:T(8,128)(2,1)} %fusion.5), calls=%async_computation.2 | async-start | bytes 2097152 | tf_op jit(solution)/shard_map/all_to_all | solution.py:96
  136.8 14.8 %copy-start.1 = (bf16[512,1024]{1,0:T(8,128)(2,1)S(1)}, bf16[512,1024]{1,0:T(8,128)(2,1)}, u32[]{:S(2)}) copy-start(bf16[512,1024]{1,0:T(8,128)(2,1)} %param.8) | copy-start | bytes 3145732
  136.8 18.4 %collective-permute-start.1 = (bf16[3,512,256]{2,1,0:T(8,128)(2,1)}, bf16[3,512,256]{2,1,0:T(8,128)(2,1)S(1)}, u32[]{:S(2)}, u32[]{:S(2)}) collective-permute-start(bf16[3,512,256]{2,1,0:T(8,128)(2,1)} %divide_convert_fusion), channel_id=1, source_target_pairs={{0,4},{4,0},{1,5},{5,1},{2,6},{6,2},{3,7},{7,3},{8,12},{12,8},{9,1... | collective-permute-start | bytes 2359304 | tf_op jit(solution)/shard_map/ppermute | solution.py:107

commit v3 on v2

--- a/solution.py
+++ b/solution.py
@@ -5,7 +5,8 @@
 from jax.sharding import PartitionSpec as P
 
 NS_ITERS = 3
-TOK = ("z", "core")
+Z = ("pair", "parity")
+TOK = ("pair", "parity", "core")
 
 poly_a = 3.4445
 poly_b = -4.775
@@ -19,6 +20,15 @@
 def sum_of_copies(pieces, axis):
     got = lax.all_to_all(pieces, axis, 0, 0, tiled=True)
     return jnp.sum(got.astype(jnp.float32), axis=0)
+
+
+def halves_by_parity(blocks, odd, dim):
+    def quarter(index):
+        return lax.dynamic_index_in_dim(blocks, index, dim, False)
+
+    kept = [quarter(2 * part + odd) for part in range(2)]
+    sent = [quarter(2 * part + 1 - odd) for part in range(2)]
+    return kept, sent
 
 
 def head_gradients(keys, values, rate, gate, up, down):
@@ -71,7 +81,13 @@
     tok_rows, all_cols = keys.shape
     width = all_cols // token_rate.shape[1]
     units = w_gate.shape[2]
-    chunk = width // lax.axis_size("z")
+    chunk = width // lax.axis_size(Z)
+    odd = lax.axis_index("parity")
+    depth = lax.axis_size(Z)
+    ways = (
+        [(at, at ^ 1) for at in range(depth)],
+        [(at, (at + (1 if at % 2 else -1)) % depth) for at in range(depth)],
+    )
     core = lax.axis_index("core")
     other = 1 - core
 
@@ -89,9 +105,28 @@
     swap = [(0, 1), (1, 0)]
     received = lax.ppermute(gradients_of(other).astype(jnp.bfloat16), "core", swap)
     summed = gradients_of(core) + received.astype(jnp.float32)
-    pieces = summed.astype(jnp.bfloat16).reshape(3, -1, chunk, units).swapaxes(0, 1)
-    owned = sum_of_copies(pieces, "z").astype(jnp.bfloat16)
-    full = lax.all_gather(owned, "z", axis=1, tiled=True)
+    summed = summed.astype(jnp.bfloat16).reshape(3, 4, width // 4, units)
+    kept, sent = halves_by_parity(summed, odd, 1)
+    pair_sum = jnp.stack(
+        [
+            kept[part].astype(jnp.float32)
+            + lax.ppermute(sent[part], Z, ways[part]).astype(jnp.float32)
+            for part in range(2)
+        ],
+        axis=1,
+    ).astype(jnp.bfloat16)
+    pieces = pair_sum.reshape(3, -1, chunk, units).swapaxes(0, 1)
+    owned = sum_of_copies(pieces, "pair").astype(jnp.bfloat16)
+    held = lax.all_gather(owned, "pair", axis=1, tiled=True).reshape(3, 2, width // 4, units)
+    brought = [lax.ppermute(held[:, part], Z, ways[part]) for part in range(2)]
+    full = jnp.stack(
+        [
+            jnp.where(odd == place, held[:, part], brought[part])
+            for part in range(2)
+            for place in range(2)
+        ],
+        axis=1,
+    ).reshape(3, width, units)
     blocks = lax.all_to_all(jnp.concatenate((full, full[:1]), axis=0), "hid", 0, 0, tiled=True)
     ortho = lax.all_to_all(newton_schulz(blocks), "hid", 0, 0, tiled=True)[:3]
 
@@ -131,8 +166,8 @@
 
 def solution(mesh):
     finer = Mesh(
-        mesh.devices.reshape(mesh.shape["head"], -1, 2, mesh.shape["hid"]),
-        ("head", "z", "core", "hid"),
+        mesh.devices.reshape(mesh.shape["head"], -1, 2, 2, mesh.shape["hid"]),
+        ("head", "pair", "parity", "core", "hid"),
     )
     return jax.shard_map(
         local,

time: 175 us -> 188 us (1.074)
  blocking collectives: 107 us -> 87 us
  starting transfers between devices: 26.1 us -> 41.5 us
  waiting for transfers between devices: 8.79 us -> 17 us
  matrix products: 20.8 us -> 26.5 us
  local copies, waits for them, and re-layouts: 4.77 us -> 7.84 us
    ppermute x0 -> x4, starting transfers between devices: none -> 15.4 us  [the longest x2 8.41 us: local(): lax.ppermute(sent[part], Z, ways[part]).astype(jnp.float32)]
    all_to_all x2, blocking collectives: 63.9 us -> 48.8 us  [sum_of_copies(): got = lax.all_to_all(pieces, axis, 0, 0, tiled=True)]
    ppermute x0 -> x4, waiting for transfers between devices: none -> 7.99 us  [the longest x2 4.96 us: local(): lax.ppermute(sent[part], Z, ways[part]).astype(jnp.float32)]
    dot_general x20, matrix products: 13.1 us -> 18.7 us  [dot32(): lax.dot_general(left, right, (contract, ((), ())), preferred_element_type...]
    all_gather x1, blocking collectives: 30 us -> 24.7 us  [local(): lax.all_gather(owned, 'pair', axis=1, tiled=True)]
    unnamed x18 -> x26, local copies, waits for them, and re-layouts: 2.86 us -> 4.89 us
  transfers between devices with their start and end apart: 3 -> 7, of which waited for: 1 -> 3; matrix products, arithmetic and copies ran while one was open for 5% -> 6% of each run, Pallas kernels for 0% -> 0%
where the time goes in v3:
time: 188 us; the launch traced here: 187 us
  blocking collectives  87 us (46%)
  starting transfers between devices  41.5 us (22%)
  matrix products  26.5 us (14%)
  waiting for transfers between devices  17 us (9%)
  local copies, waits for them, and re-layouts  7.84 us (4%)
  other arithmetic  5.97 us (3%)
    all_to_all x2, blocking collectives, sum_of_copies(): got = lax.all_to_all(pieces, axis, 0, 0, tiled=True)  48.8 us
    all_gather x1, blocking collectives, local(): lax.all_gather(owned, 'pair', axis=1, tiled=True)  24.7 us
    dot_general x20, matrix products, dot32(): lax.dot_general(left, right, (contract, ((), ())), preferred_element_type...  18.7 us
    ppermute x1, starting transfers between devices, local(): theirs = lax.ppermute(mine, 'core', swap)  13.7 us
    all_to_all x1, blocking collectives, local(): lax.all_to_all(jnp.concatenate((full, full[:1]), axis=0), 'hid', 0, 0, ti...  13.6 us
    all_to_all x1, waiting for transfers between devices, local(): ortho = lax.all_to_all(newton_schulz(blocks), 'hid', 0, 0, tiled=True)[:3]  8.97 us
    ppermute x1, starting transfers between devices, local(): lax.ppermute(gradients_of(other).astype(jnp.bfloat16), 'core', swap)  8.76 us
    ppermute x2, starting transfers between devices, local(): lax.ppermute(sent[part], Z, ways[part]).astype(jnp.float32)  8.41 us
  transfers between devices with their start and end apart: 7, of which 3 were waited for; matrix products, arithmetic and copies ran while one was open for 6% of the time, Pallas kernels for 0%

profile of v3, /device:TPU:1, one launch (start us, length us, event | category | flops | bytes accessed | tf_op | source)
XLA Modules:
  0.0 187.0 jit_solution(13337647702683237891)
XLA Ops:
  0.0 1.2 copy-done
  1.2 1.3 fusion.42
  2.6 0.3 fusion.44
  2.9 1.4 fusion.56
  4.3 0.5 fusion.21
  4.8 0.5 fusion.20
  5.3 0.7 copy-done.8
  6.0 0.6 fusion.22
  6.6 0.1 pad_maximum_fusion.3
  6.7 8.8 %collective-permute-start = (bf16[3,512,256]{2,1,0:T(8,128)(2,1)S(1)}, bf16[3,512,256]{2,1,0:T(8,128)(2,1)S(1)}, u32[]{:S(2)}, u32[]{:S(2)}) collective-permute-start(bf16[3,512,256]{2,1,0:T(8,128)(2,1)S(1)} %pad_maximum_fusion.3), channel_id=1, source_target_pairs={{0,4},{4,0},{1,5},{5,1},{2,6},{6,2},{3,7},{7,3},{8,12},{12,8},{9,1... | collective-permute-start | bytes 2359304 | tf_op jit(solution)/shard_map/ppermute | solution.py:106
  15.4 1.0 constant_dynamic-slice_fusion.2
  16.4 1.1 constant_dynamic-slice_fusion.3
  17.5 0.3 fusion.48
  17.8 0.9 copy-done.9
  18.7 0.3 fusion.52
  19.1 0.8 copy-done.11
  19.9 1.3 convolution_bitcast_fusion.4
  21.2 0.3 fusion.50
  21.5 0.7 copy-done.3
  22.2 1.6 convolution_bitcast_fusion.3
  23.9 0.5 convolution_bitcast_fusion.5
  24.4 0.5 copy-done.5
  24.9 0.2 fusion.8
  25.2 1.9 %collective-permute-start.1 = (bf16[3,128,256]{2,1,0:T(8,128)(2,1)S(1)}, bf16[3,128,256]{2,1,0:T(8,128)(2,1)S(1)}, u32[]{:S(2)}, u32[]{:S(2)}) collective-permute-start(bf16[3,128,256]{2,1,0:T(8,128)(2,1)S(1)} %get-tuple-element.11), channel_id=1, source_target_pairs={{0,8},{8,0},{16,24},{24,16},{32,40},{40,32},{48,56},{56,48},{64,72... | collective-permute-start | bytes 589832 | tf_op jit(solution)/shard_map/ppermute | solution.py:113
  27.1 6.5 %collective-permute-start.2 = (bf16[3,128,256]{2,1,0:T(8,128)(2,1)S(1)}, bf16[3,128,256]{2,1,0:T(8,128)(2,1)S(1)}, u32[]{:S(2)}, u32[]{:S(2)}) collective-permute-start(bf16[3,128,256]{2,1,0:T(8,128)(2,1)S(1)} %get-tuple-element.12), channel_id=1, source_target_pairs={{0,120},{8,16},{16,8},{24,32},{32,24},{40,48},{48,40},{56,64},{64,... | collective-permute-start | bytes 589832 | tf_op jit(solution)/shard_map/ppermute | solution.py:113
  33.6 5.0 %collective-permute-done.2 = bf16[3,128,256]{2,1,0:T(8,128)(2,1)S(1)} collective-permute-done((bf16[3,128,256]{2,1,0:T(8,128)(2,1)S(1)}, bf16[3,128,256]{2,1,0:T(8,128)(2,1)S(1)}, u32[]{:S(2)}, u32[]{:S(2)}) %collective-permute-start.2) | collective-permute-done | bytes 196640 | tf_op jit(solution)/shard_map/ppermute | solution.py:113
  38.6 0.1 fusion.64
  38.8 31.4 %all_to_all.20 = bf16[8,3,32,256]{3,2,1,0:T(8,128)(2,1)S(1)} all-to-all(bf16[8,3,32,256]{3,2,1,0:T(8,128)(2,1)S(1)} %copy.46), channel_id=1, replica_groups=mesh['head'=4,'pair'=8,'parity'=2,'core'=2,'hid'=4] {'pair'}, dimensions={0} | all-to-all | bytes 786432 | tf_op jit(solution)/shard_map/all_to_all | solution.py:21
  70.3 24.7 %all_gather.3 = bf16[3,256,256]{2,1,0:T(8,128)(2,1)S(1)} all-gather(bf16[3,32,256]{2,1,0:T(8,128)(2,1)S(1)} %reduce_sum.51), channel_id=1, replica_groups=mesh['head'=4,'pair'=8,'parity'=2,'core'=2,'hid'=4] {'pair'}, dimensions={1}, use_global_device_ids=true | all-gather | bytes 442368 | tf_op jit(solution)/shard_map/all_gather | solution.py:120
  95.0 1.9 %collective-permute-start.3 = (bf16[3,128,256]{2,1,0:T(8,128)(2,1)S(1)}, bf16[3,128,256]{2,1,0:T(8,128)(2,1)S(1)}, u32[]{:S(2)}, u32[]{:S(2)}) collective-permute-start(bf16[3,128,256]{2,1,0:T(8,128)(2,1)S(1)} %get-tuple-element.19), channel_id=1, source_target_pairs={{0,8},{8,0},{16,24},{24,16},{32,40},{40,32},{48,56},{56,48},{64,72... | collective-permute-start | bytes 589832 | tf_op jit(solution)/shard_map/ppermute | solution.py:121
  96.9 5.0 %collective-permute-start.4 = (bf16[3,128,256]{2,1,0:T(8,128)(2,1)S(1)}, bf16[3,128,256]{2,1,0:T(8,128)(2,1)S(1)}, u32[]{:S(2)}, u32[]{:S(2)}) collective-permute-start(bf16[3,128,256]{2,1,0:T(8,128)(2,1)S(1)} %get-tuple-element.20), channel_id=1, source_target_pairs={{0,120},{8,16},{16,8},{24,32},{32,24},{40,48},{48,40},{56,64},{64,... | collective-permute-start | bytes 589832 | tf_op jit(solution)/shard_map/ppermute | solution.py:121
  102.0 3.0 %collective-permute-done.4 = bf16[3,128,256]{2,1,0:T(8,128)(2,1)S(1)} collective-permute-done((bf16[3,128,256]{2,1,0:T(8,128)(2,1)S(1)}, bf16[3,128,256]{2,1,0:T(8,128)(2,1)S(1)}, u32[]{:S(2)}, u32[]{:S(2)}) %collective-permute-start.4) | collective-permute-done | bytes 196640 | tf_op jit(solution)/shard_map/ppermute | solution.py:121
  105.1 0.1 pad_maximum_fusion.4
  105.3 0.1 pad_maximum_fusion
  105.4 13.6 %all_to_all.21 = bf16[4,512,256]{2,1,0:T(8,128)(2,1)S(1)} all-to-all(bf16[4,512,256]{2,1,0:T(8,128)(2,1)S(1)} %pad_maximum_fusion), channel_id=1, replica_groups=mesh['head'=4,'pair'=8,'parity'=2,'core'=2,'hid'=4] {'hid'}, dimensions={0} | all-to-all | bytes 2097152 | tf_op jit(solution)/shard_map/all_to_all | solution.py:130
  119.0 1.1 fusion
  120.8 0.7 fusion.18
  121.6 0.7 fusion.9
  122.3 0.8 fusion.4
  123.1 0.7 fusion.17
  123.9 0.7 fusion.11
  124.6 0.8 fusion.6
  125.4 0.7 fusion.16
  126.2 0.7 fusion.12
  126.9 1.8 fusion.5
  128.7 3.6 %all-to-all-start.2 = ((bf16[4,512,256]{2,1,0:T(8,128)(2,1)}), bf16[4,512,256]{2,1,0:T(8,128)(2,1)S(1)}, u32[]{:S(2)}, u32[]{:S(2)}) async-start(bf16[4,512,256]{2,1,0:T(8,128)(2,1)} %fusion.5), calls=%async_computation.2 | async-start | bytes 2097152 | tf_op jit(solution)/shard_map/all_to_all | solution.py:131
  132.3 0.1 copy.43
  132.5 0.6 dynamic_slice.68
  133.1 9.0 %all-to-all-done.2 = bf16[4,512,256]{2,1,0:T(8,128)(2,1)S(1)} async-done(((bf16[4,512,256]{2,1,0:T(8,128)(2,1)}), bf16[4,512,256]{2,1,0:T(8,128)(2,1)S(1)}, u32[]{:S(2)}, u32[]{:S(2)}) %all-to-all-start.2) | async-done | bytes 1048608 | tf_op jit(solution)/shard_map/all_to_all | solution.py:131
  142.0 1.1 fusion.7
  143.1 1.9 %divide_convert_fusion = bf16[3,512,256]{2,1,0:T(8,128)(2,1)} fusion(f32[3,256]{1,0:T(4,128)S(1)} %add_sqrt_fusion, f32[3,256]{1,0:T(4,128)S(1)} %sqrt.20, f32[]{:T(128)} %bitcast.3, bf16[4,512,256]{2,1,0:T(8,128)(2,1)S(1)} %all-to-all-done.2, bf16[1,512,256]{2,1,0:T(8,128)(2,1)S(1)} %bitcast.187, bf16[1,512,256]{2,1,0:T(8,128)(2,1)S(1)} %get-tuple-element.23, ...), kind=kLoop, calls=%fused_computation.17 | loop fusion | flops 3538944 | bytes 2365444 | tf_op jit(solution)/shard_map/convert_element_type | solution.py:77
  145.0 13.7 %collective-permute-start.5 = (bf16[3,512,256]{2,1,0:T(8,128)(2,1)}, bf16[3,512,256]{2,1,0:T(8,128)(2,1)}, u32[]{:S(2)}, u32[]{:S(2)}) collective-permute-start(bf16[3,512,256]{2,1,0:T(8,128)(2,1)} %divide_convert_fusion), channel_id=1, source_target_pairs={{0,4},{4,0},{1,5},{5,1},{2,6},{6,2},{3,7},{7,3},{8,12},{12,8},{9,1... | collective-permute-start | bytes 2359304 | tf_op jit(solution)/shard_map/ppermute | solution.py:142
  158.7 1.4 fusion.36
  160.1 1.3 fusion.19
  161.4 1.2 fusion.23
  162.6 1.2 fusion.24
  163.7 1.3 fusion.31
  165.0 1.3 multiply_convert_fusion.1
  166.3 1.2 fusion.25
  167.4 1.2 fusion.26
  168.6 0.1 broadcast_select_fusion.1
  168.7 0.1 pad_maximum_fusion.1
  168.8 17.3 %all_to_all.22 = bf16[4,512,256]{2,1,0:T(8,128)(2,1)S(1)} all-to-all(bf16[4,512,256]{2,1,0:T(8,128)(2,1)S(1)} %pad_maximum_fusion.1), channel_id=1, replica_groups=mesh['head'=4,'pair'=8,'parity'=2,'core'=2,'hid'=4] {'hid'}, dimensions={0} | all-to-all | bytes 2097152 | tf_op jit(solution)/shard_map/all_to_all | solution.py:21
  186.1 0.9 reduce_sum.55
  (35 shorter events, 0.4 us)
Async XLA Ops:
  0.0 1.2 copy-start
  0.0 2.5 %copy-start.4 = (bf16[2,512,256]{2,1,0:T(8,128)(2,1)S(1)}, bf16[2,512,256]{2,1,0:T(8,128)(2,1)}, u32[]{:S(2)}) copy-start(bf16[2,512,256]{2,1,0:T(8,128)(2,1)} %param.14) | copy-start | bytes 1572868
  1.2 1.6 copy-start.7
  1.2 1.7 copy-start.6
  4.8 1.2 copy-start.8
  6.7 17.7 %collective-permute-start = (bf16[3,512,256]{2,1,0:T(8,128)(2,1)S(1)}, bf16[3,512,256]{2,1,0:T(8,128)(2,1)S(1)}, u32[]{:S(2)}, u32[]{:S(2)}) collective-permute-start(bf16[3,512,256]{2,1,0:T(8,128)(2,1)S(1)} %pad_maximum_fusion.3), channel_id=1, source_target_pairs={{0,4},{4,0},{1,5},{5,1},{2,6},{6,2},{3,7},{7,3},{8,12},{12,8},{9,1... | collective-permute-start | bytes 2359304 | tf_op jit(solution)/shard_map/ppermute | solution.py:106
  17.5 1.2 copy-start.9
  17.8 1.3 copy-start.2
  19.1 0.8 copy-start.11
  21.2 1.0 copy-start.3
  22.2 1.6 copy-start.12
  23.9 1.0 copy-start.5
  25.2 8.4 %collective-permute-start.1 = (bf16[3,128,256]{2,1,0:T(8,128)(2,1)S(1)}, bf16[3,128,256]{2,1,0:T(8,128)(2,1)S(1)}, u32[]{:S(2)}, u32[]{:S(2)}) collective-permute-start(bf16[3,128,256]{2,1,0:T(8,128)(2,1)S(1)} %get-tuple-element.11), channel_id=1, source_target_pairs={{0,8},{8,0},{16,24},{24,16},{32,40},{40,32},{48,56},{56,48},{64,72... | collective-permute-start | bytes 589832 | tf_op jit(solution)/shard_map/ppermute | solution.py:113
  27.1 11.5 %collective-permute-start.2 = (bf16[3,128,256]{2,1,0:T(8,128)(2,1)S(1)}, bf16[3,128,256]{2,1,0:T(8,128)(2,1)S(1)}, u32[]{:S(2)}, u32[]{:S(2)}) collective-permute-start(bf16[3,128,256]{2,1,0:T(8,128)(2,1)S(1)} %get-tuple-element.12), channel_id=1, source_target_pairs={{0,120},{8,16},{16,8},{24,32},{32,24},{40,48},{48,40},{56,64},{64,... | collective-permute-start | bytes 589832 | tf_op jit(solution)/shard_map/ppermute | solution.py:113
  95.0 7.0 %collective-permute-start.3 = (bf16[3,128,256]{2,1,0:T(8,128)(2,1)S(1)}, bf16[3,128,256]{2,1,0:T(8,128)(2,1)S(1)}, u32[]{:S(2)}, u32[]{:S(2)}) collective-permute-start(bf16[3,128,256]{2,1,0:T(8,128)(2,1)S(1)} %get-tuple-element.19), channel_id=1, source_target_pairs={{0,8},{8,0},{16,24},{24,16},{32,40},{40,32},{48,56},{56,48},{64,72... | collective-permute-start | bytes 589832 | tf_op jit(solution)/shard_map/ppermute | solution.py:121
  96.9 8.1 %collective-permute-start.4 = (bf16[3,128,256]{2,1,0:T(8,128)(2,1)S(1)}, bf16[3,128,256]{2,1,0:T(8,128)(2,1)S(1)}, u32[]{:S(2)}, u32[]{:S(2)}) collective-permute-start(bf16[3,128,256]{2,1,0:T(8,128)(2,1)S(1)} %get-tuple-element.20), channel_id=1, source_target_pairs={{0,120},{8,16},{16,8},{24,32},{32,24},{40,48},{48,40},{56,64},{64,... | collective-permute-start | bytes 589832 | tf_op jit(solution)/shard_map/ppermute | solution.py:121
  128.7 3.8 %copy-start.10 = (f32[2]{0:T(128)S(1)}, f32[2]{0:T(128)}, u32[]{:S(2)}) copy-start(f32[2]{0:T(128)} %param.12) | copy-start | bytes 28
  128.7 13.4 %all-to-all-start.2 = ((bf16[4,512,256]{2,1,0:T(8,128)(2,1)}), bf16[4,512,256]{2,1,0:T(8,128)(2,1)S(1)}, u32[]{:S(2)}, u32[]{:S(2)}) async-start(bf16[4,512,256]{2,1,0:T(8,128)(2,1)} %fusion.5), calls=%async_computation.2 | async-start | bytes 2097152 | tf_op jit(solution)/shard_map/all_to_all | solution.py:131
  145.0 15.1 %copy-start.1 = (bf16[512,1024]{1,0:T(8,128)(2,1)S(1)}, bf16[512,1024]{1,0:T(8,128)(2,1)}, u32[]{:S(2)}) copy-start(bf16[512,1024]{1,0:T(8,128)(2,1)} %param.8) | copy-start | bytes 3145732
  145.0 18.7 %collective-permute-start.5 = (bf16[3,512,256]{2,1,0:T(8,128)(2,1)}, bf16[3,512,256]{2,1,0:T(8,128)(2,1)}, u32[]{:S(2)}, u32[]{:S(2)}) collective-permute-start(bf16[3,512,256]{2,1,0:T(8,128)(2,1)} %divide_convert_fusion), channel_id=1, source_target_pairs={{0,4},{4,0},{1,5},{5,1},{2,6},{6,2},{3,7},{7,3},{8,12},{12,8},{9,1... | collective-permute-start | bytes 2359304 | tf_op jit(solution)/shard_map/ppermute | solution.py:142

commit v4 on v2

v4 whole, which is shorter than its diff:
```python
import jax
import jax.numpy as jnp
from jax import lax
from jax.experimental import pallas as pl
from jax.experimental.pallas import tpu as pltpu
from jax.sharding import Mesh
from jax.sharding import PartitionSpec as P

NS_ITERS = 3
TOK = ("z", "core")
KINDS = 3
TILE = 128

poly_a = 3.4445
poly_b = -4.775
poly_c = 2.0315


def dot32(left, right, contract):
    return lax.dot_general(left, right, (contract, ((), ())), preferred_element_type=jnp.float32)


def sum_of_copies(pieces, axis):
    got = lax.all_to_all(pieces, axis, 0, 0, tiled=True)
    return jnp.sum(got.astype(jnp.float32), axis=0)


def sigmoid(value):
    return 1.0 / (1.0 + jnp.exp(-value))


def gradients_kernel(head_ref, keys, values, rate, gate, up, down, out, target, d_gate, d_up, hidden):
    first = head_ref[0] == 0
    rows = keys.shape[0]
    for start in range(0, rows, TILE):
        part = slice(start, start + TILE)
        own_rate = jnp.where(first, rate[part, 0:1], rate[part, 1:2])
        goal = (-(own_rate * values[part, :].astype(jnp.float32))).astype(jnp.bfloat16)
        target[part, :] = goal
        gate_pre = dot32(keys[part, :], gate[0], ((1,), (0,)))
        up_pre = dot32(keys[part, :], up[0], ((1,), (0,)))
        back = dot32(goal, down[0], ((1,), (1,)))
        gate_sig = sigmoid(gate_pre)
        active = gate_pre * gate_sig
        hidden[part, :] = (active * up_pre).astype(jnp.bfloat16)
        d_gate[part, :] = (back * up_pre * gate_sig * (1.0 + gate_pre * (1.0 - gate_sig))).astype(
            jnp.bfloat16
        )
        d_up[part, :] = (back * active).astype(jnp.bfloat16)
    depth, _, chunk, units = out.shape
    for kind, (left, right) in enumerate(((keys, d_gate), (keys, d_up), (target, hidden))):
        term = dot32(left[...], right[...], ((0,), (0,))).astype(jnp.bfloat16)
        out[:, kind] = term.reshape(depth, chunk, units)


def newton_schulz_kernel(blocks, out, iterate, product, gram, raw):
    count, rows, units = blocks.shape
    columns = [slice(at * units, (at + 1) * units) for at in range(count)]
    halves = [slice(at, at + units) for at in range(0, rows, units)]
    for at in range(count):
        iterate[:, columns[at]] = blocks[at]
    scale = None
    for iteration in range(NS_ITERS):
        if iteration == 0:
            trace = jnp.zeros((1, 1), jnp.float32)
            for half in halves:
                block = dot32(iterate[...], iterate[half, :], ((1,), (1,)))
                raw[:, half] = block
                square = block[half, :]
                line = lax.broadcasted_iota(jnp.int32, square.shape, 0)
                column = lax.broadcasted_iota(jnp.int32, square.shape, 1)
                trace = trace + jnp.sum(
                    jnp.where(line == column, square, 0.0), axis=(0, 1), keepdims=True
                )
            scale = 1.0 / (jnp.sqrt(trace) + 1e-07)
            for half in halves:
                gram[:, half] = (raw[:, half] * (scale * scale)).astype(jnp.bfloat16)
        else:
            for half in halves:
                gram[:, half] = dot32(iterate[...], iterate[half, :], ((1,), (1,))).astype(
                    jnp.bfloat16
                )
        for at in range(count):
            block = dot32(gram[...], iterate[:, columns[at]], ((1,), (0,)))
            if iteration == 0:
                block = block * scale
            product[:, columns[at]] = block.astype(jnp.bfloat16)
        for at in range(count):
            second = dot32(gram[...], product[:, columns[at]], ((1,), (0,)))
            leading = iterate[:, columns[at]].astype(jnp.float32)
            if iteration == 0:
                leading = leading * scale
            block = (
                poly_a * leading
                + poly_b * product[:, columns[at]].astype(jnp.float32)
                + poly_c * second
            ).astype(jnp.bfloat16)
            if iteration == NS_ITERS - 1:
                out[at] = block
            else:
                iterate[:, columns[at]] = block


def rescale_kernel(head_ref, head_rate, ortho, gate, up, down, out):
    step = head_rate[head_ref[0]]
    for kind in range(KINDS):
        if kind == 2:
            old = down[0].astype(jnp.float32).T
        else:
            old = (gate, up)[kind][0].astype(jnp.float32)
        fresh = old - step * ortho[kind].astype(jnp.float32)
        old_norm = jnp.sqrt(jnp.sum(old * old, axis=0, keepdims=True))
        new_norm = jnp.sqrt(jnp.sum(fresh * fresh, axis=0, keepdims=True) + 1e-06)
        out[kind] = (fresh * (old_norm / new_norm)).astype(jnp.bfloat16)


def query_kernel(head_ref, queries, weights, *rest):
    out = rest[-1]
    half = out.shape[2]
    rows = queries.shape[0]
    for start in range(0, rows, 2 * TILE):
        part = slice(start, start + 2 * TILE)
        query_gate = dot32(queries[part, :], weights[0], ((1,), (0,)))
        query_up = dot32(queries[part, :], weights[1], ((1,), (0,)))
        query_hidden = (query_gate * sigmoid(query_gate) * query_up).astype(jnp.bfloat16)
        for at in range(out.shape[0]):
            features = weights[2, at * half : (at + 1) * half, :]
            out[at, part, :] = dot32(query_hidden, features, ((1,), (1,))).astype(jnp.bfloat16)


def cost(flops, operands):
    return pl.CostEstimate(flops=flops, transcendentals=0, bytes_accessed=operands)


def gradients_of(head, keys, values, rate, gate, up, down, depth):
    rows, width = keys.shape[0], gate.shape[1]
    units = gate.shape[2]
    columns = pl.BlockSpec((rows, width), lambda step, head: (0, head[0]))
    weight = pl.BlockSpec((1, width, units), lambda step, head: (head[0], 0, 0))
    return pl.pallas_call(
        gradients_kernel,
        grid_spec=pltpu.PrefetchScalarGridSpec(
            num_scalar_prefetch=1,
            grid=(1,),
            in_specs=[
                columns,
                columns,
                pl.BlockSpec(rate.shape, lambda step, head: (0, 0)),
                weight,
                weight,
                pl.BlockSpec((1, units, width), lambda step, head: (head[0], 0, 0)),
            ],
            out_specs=pl.BlockSpec(
                (depth, KINDS, width // depth, units), lambda step, head: (0, 0, 0, 0)
            ),
            scratch_shapes=[
                pltpu.VMEM((rows, width), jnp.bfloat16),
                pltpu.VMEM((rows, units), jnp.bfloat16),
                pltpu.VMEM((rows, units), jnp.bfloat16),
                pltpu.VMEM((rows, units), jnp.bfloat16),
            ],
        ),
        out_shape=jax.ShapeDtypeStruct((depth, KINDS, width // depth, units), jnp.bfloat16),
        cost_estimate=cost(12 * rows * width * units, 4 * rows * width),
        name="gradients",
    )(head, keys, values, rate, gate, up, down)


def newton_schulz(blocks):
    count, rows, units = blocks.shape
    return pl.pallas_call(
        newton_schulz_kernel,
        out_shape=jax.ShapeDtypeStruct(blocks.shape, blocks.dtype),
        scratch_shapes=[
            pltpu.VMEM((rows, count * units), jnp.bfloat16),
            pltpu.VMEM((rows, count * units), jnp.bfloat16),
            pltpu.VMEM((rows, rows), jnp.bfloat16),
            pltpu.VMEM((rows, rows), jnp.float32),
        ],
        cost_estimate=cost(18 * rows * rows * count * units, 4 * blocks.size),
        name="newton_schulz",
    )(blocks)


def rescaled(head, head_rate, ortho, gate, up, down):
    _, width, units = gate.shape
    weight = pl.BlockSpec((1, width, units), lambda step, head: (head[0], 0, 0))
    return pl.pallas_call(
        rescale_kernel,
        grid_spec=pltpu.PrefetchScalarGridSpec(
            num_scalar_prefetch=1,
            grid=(1,),
            in_specs=[
                pl.BlockSpec(memory_space=pltpu.SMEM),
                pl.BlockSpec((KINDS, width, units), lambda step, head: (0, 0, 0)),
                weight,
                weight,
                pl.BlockSpec((1, units, width), lambda step, head: (head[0], 0, 0)),
            ],
            out_specs=pl.BlockSpec((KINDS, width, units), lambda step, head: (0, 0, 0)),
        ),
        out_shape=jax.ShapeDtypeStruct((KINDS, width, units), jnp.bfloat16),
        cost_estimate=cost(20 * KINDS * width * units, 6 * KINDS * width * units),
        name="rescale",
    )(head, head_rate, ortho, gate, up, down)


def query_terms(head, queries, weights, earlier=None):
    rows = queries.shape[0]
    _, width, units = weights.shape
    pieces = width // units
    shape = jax.ShapeDtypeStruct((2 * pieces, rows, units), jnp.bfloat16)
    return pl.pallas_call(
        query_kernel,
        grid_spec=pltpu.PrefetchScalarGridSpec(
            num_scalar_prefetch=1,
            grid=(1,),
            in_specs=[
                pl.BlockSpec((rows, width), lambda step, head: (0, head[0])),
                pl.BlockSpec(weights.shape, lambda step, head: (0, 0, 0)),
            ]
            + ([] if earlier is None else [pl.BlockSpec(memory_space=pl.ANY)]),
            out_specs=pl.BlockSpec((pieces, rows, units), lambda step, head: (head[0], 0, 0)),
        ),
        out_shape=shape,
        input_output_aliases={} if earlier is None else {3: 0},
        cost_estimate=cost(6 * rows * width * units, 4 * rows * width),
        name="query",
    )(head, queries, weights, *(() if earlier is None else (earlier,)))


def local(queries, keys, values, token_rate, head_rate, w_gate, w_up, w_down):
    core = lax.axis_index("core").astype(jnp.int32)
    mine, theirs = core.reshape(1), (1 - core).reshape(1)
    swap = [(0, 1), (1, 0)]
    given = (keys, values, token_rate, w_gate, w_up, w_down, lax.axis_size("z"))
    received = lax.ppermute(gradients_of(theirs, *given), "core", swap)
    pieces = (
        gradients_of(mine, *given).astype(jnp.float32) + received.astype(jnp.float32)
    ).astype(jnp.bfloat16)
    owned = sum_of_copies(pieces, "z").astype(jnp.bfloat16)
    full = lax.all_gather(owned, "z", axis=1, tiled=True)
    blocks = lax.all_to_all(jnp.concatenate((full, full[:1]), axis=0), "hid", 0, 0, tiled=True)
    ortho = lax.all_to_all(newton_schulz(blocks), "hid", 0, 0, tiled=True)
    new = rescaled(mine, head_rate, ortho, w_gate, w_up, w_down)
    new_there = lax.ppermute(new, "core", swap)
    terms = query_terms(theirs, queries, new_there, query_terms(mine, queries, new))
    return sum_of_copies(terms, "hid").astype(jnp.bfloat16)


def solution(mesh):
    finer = Mesh(
        mesh.devices.reshape(mesh.shape["head"], -1, 2, mesh.shape["hid"]),
        ("head", "z", "core", "hid"),
    )
    return jax.shard_map(
        local,
        mesh=finer,
        in_specs=(
            P(TOK, "head"),
            P(TOK, "head"),
            P(TOK, "head"),
            P(TOK, "head"),
            P("head"),
            P("head", None, "hid"),
            P("head", None, "hid"),
            P("head", "hid", None),
        ),
        out_specs=P(TOK, ("head", "hid")),
        check_vma=False,
    )
```

time: 175 us -> 175 us (level)
  Pallas kernels: 0 us -> 24.5 us
  matrix products: 20.8 us -> 0 us
  blocking collectives: 107 us -> 122 us
  waiting for transfers between devices: 8.79 us -> 0.01 us
  starting transfers between devices: 26.1 us -> 22.5 us
  other arithmetic: 5.73 us -> 2.55 us
  local copies, waits for them, and re-layouts: 4.77 us -> 2.48 us
    pallas_call x0 -> x6, Pallas kernels: none -> 24.5 us  [the longest x1 8.1 us: newton_schulz(): pl.pallas_call(newton_schulz_kernel, out_shape=jax.ShapeDtypeStruct(block...]
    dot_general x29 -> x0, matrix products: 20.8 us -> none  [the longest x20 13.1 us: dot32(): lax.dot_general(left, right, (contract, ((), ())), preferred_element_type...]
    all_to_all x0 -> x1, blocking collectives: none -> 14.1 us  [local(): ortho = lax.all_to_all(newton_schulz(blocks), 'hid', 0, 0, tiled=True)]
    all_to_all x1 -> x0, waiting for transfers between devices: 8.79 us -> none  [local(): ortho = lax.all_to_all(newton_schulz(blocks), 'hid', 0, 0, tiled=True)[:3]]
    all_to_all x1 -> x0, starting transfers between devices: 3.83 us -> none  [local(): ortho = lax.all_to_all(newton_schulz(blocks), 'hid', 0, 0, tiled=True)[:3]]
    reduce_sum x2 -> x0, other arithmetic: 2.21 us -> none  [the longest x1 1.14 us: newton_schulz(): sq_norm = jnp.sum(jnp.square(blocks.astype(jnp.float32)))]
    dynamic_slice x5 -> x0, local copies, waits for them, and re-layouts: 1.83 us -> none  [the longest x1 1.07 us: local(): lax.dynamic_index_in_dim(w_up, core, 0, False)]
  transfers between devices with their start and end apart: 3 -> 2, of which waited for: 1 -> 0; matrix products, arithmetic and copies ran while one was open for 5% -> 0% of each run, Pallas kernels for 0% -> 4%
where the time goes in v4:
time: 175 us; the launch traced here: 174 us
  blocking collectives  122 us (70%)
  Pallas kernels  24.5 us (14%)
  starting transfers between devices  22.5 us (13%)
  other arithmetic  2.55 us (1%)
  local copies, waits for them, and re-layouts  2.48 us (1%)
    all_to_all x2, blocking collectives, sum_of_copies(): got = lax.all_to_all(pieces, axis, 0, 0, tiled=True)  64.9 us
    all_gather x1, blocking collectives, local(): full = lax.all_gather(owned, 'z', axis=1, tiled=True)  29.3 us
    all_to_all x1, blocking collectives, local(): ortho = lax.all_to_all(newton_schulz(blocks), 'hid', 0, 0, tiled=True)  14.1 us
    all_to_all x1, blocking collectives, local(): lax.all_to_all(jnp.concatenate((full, full[:1]), axis=0), 'hid', 0, 0, ti...  13.9 us
    ppermute x1, starting transfers between devices, local(): new_there = lax.ppermute(new, 'core', swap)  13.6 us
    ppermute x1, starting transfers between devices, local(): received = lax.ppermute(gradients_of(theirs, *given), 'core', swap)  8.84 us
    pallas_call x1, Pallas kernels, newton_schulz(): pl.pallas_call(newton_schulz_kernel, out_shape=jax.ShapeDtypeStruct(block...  8.1 us
    pallas_call x2, Pallas kernels, gradients_of(): pl.pallas_call(gradients_kernel, grid_spec=pltpu.PrefetchScalarGridSpec(n...  7.85 us
  transfers between devices with their start and end apart: 2, of which 0 were waited for; matrix products, arithmetic and copies ran while one was open for 0% of the time, Pallas kernels for 4%

profile of v4, /device:TPU:1, one launch (start us, length us, event | category | flops | bytes accessed | tf_op | source)
XLA Modules:
  0.0 174.2 jit_solution(17419916118435430196)
XLA Ops:
  0.0 1.5 copy.10.rate
  1.5 3.9 %gradients.3 = bf16[16,3,32,256]{3,2,1,0:T(8,128)(2,1)} custom-call(s32[1]{0:T(128)} %bitcast.head_ref, bf16[512,1024]{1,0:T(8,128)(2,1)} %keys.3, bf16[512,1024]{1,0:T(8,128)(2,1)} %values.3, f32[512,2]{1,0:T(8,128)} %copy.10.rate, bf16[2,512,256]{2,1,0:T(8,128)(2,1)} %gate.5, bf16[2,512,256]{2,1,0:T(8,128)(2,1)} %up.5, bf16[2,256,512]{2,1,0:T(8,128)(2,1)} %down.5), custom_call_target="tpu_custom_call" | custom-call | flops 805306368 | bytes 1048576 | tf_op jit(solution)/shard_map/gradients/pallas_call | solution.py:140
  5.4 8.8 %collective-permute-start = (bf16[16,3,32,256]{3,2,1,0:T(8,128)(2,1)}, bf16[16,3,32,256]{3,2,1,0:T(8,128)(2,1)S(1)}, u32[]{:S(2)}, u32[]{:S(2)}) collective-permute-start(bf16[16,3,32,256]{3,2,1,0:T(8,128)(2,1)} %gradients.3), channel_id=1, source_target_pairs={{0,4},{4,0},{1,5},{5,1},{2,6},{6,2},{3,7},{7,3},{8,12},{12,8},{9,1... | collective-permute-start | bytes 2359304 | tf_op jit(solution)/shard_map/ppermute | solution.py:237
  14.2 4.0 %gradients.2 = bf16[16,3,32,256]{3,2,1,0:T(8,128)(2,1)} custom-call(s32[1]{0:T(128)} %bitcast.1.head_ref, bf16[512,1024]{1,0:T(8,128)(2,1)} %keys.3, bf16[512,1024]{1,0:T(8,128)(2,1)} %values.3, f32[512,2]{1,0:T(8,128)} %copy.10.rate, bf16[2,512,256]{2,1,0:T(8,128)(2,1)} %gate.5, bf16[2,512,256]{2,1,0:T(8,128)(2,1)} %up.5, bf16[2,256,512]{2,1,0:T(8,128)(2,1)} %down.5), custom_call_target="tpu_custom_call" | custom-call | flops 805306368 | bytes 1048576 | tf_op jit(solution)/shard_map/gradients/pallas_call | solution.py:140
  18.2 0.0 collective-permute-done
  18.2 1.4 add_convert_fusion
  19.7 46.5 %all_to_all.20 = bf16[16,3,32,256]{3,2,1,0:T(8,128)(2,1)S(1)} all-to-all(bf16[16,3,32,256]{3,2,1,0:T(8,128)(2,1)S(1)} %add_convert_fusion), channel_id=1, replica_groups=mesh['head'=4,'z'=16,'core'=2,'hid'=4] {'z'}, dimensions={0} | all-to-all | bytes 1572864 | tf_op jit(solution)/shard_map/all_to_all | solution.py:24
  66.2 0.1 reduce_sum.24
  66.3 29.3 %all_gather.3 = bf16[3,512,256]{2,1,0:T(8,128)(2,1)S(1)} all-gather(bf16[3,32,256]{2,1,0:T(8,128)(2,1)S(1)} %reduce_sum.24), channel_id=1, replica_groups=mesh['head'=4,'z'=16,'core'=2,'hid'=4] {'z'}, dimensions={1}, use_global_device_ids=true | all-gather | bytes 835584 | tf_op jit(solution)/shard_map/all_gather | solution.py:242
  95.6 0.1 pad_maximum_fusion
  95.7 13.9 %all_to_all.21.blocks = bf16[4,512,256]{2,1,0:T(8,128)(2,1)} all-to-all(bf16[4,512,256]{2,1,0:T(8,128)(2,1)S(1)} %pad_maximum_fusion), channel_id=1, replica_groups=mesh['head'=4,'z'=16,'core'=2,'hid'=4] {'hid'}, dimensions={0} | all-to-all | bytes 2097152 | tf_op jit(solution)/shard_map/all_to_all | solution.py:243
  109.6 8.1 %newton_schulz.1 = bf16[4,512,256]{2,1,0:T(8,128)(2,1)} custom-call(bf16[4,512,256]{2,1,0:T(8,128)(2,1)} %all_to_all.21.blocks), custom_call_target="tpu_custom_call" | custom-call | flops 4831838208 | bytes 2097152 | tf_op jit(solution)/shard_map/newton_schulz/pallas_call | solution.py:171
  117.7 14.1 %all_to_all.22.ortho = bf16[4,512,256]{2,1,0:T(8,128)(2,1)} all-to-all(bf16[4,512,256]{2,1,0:T(8,128)(2,1)} %newton_schulz.1), channel_id=1, replica_groups=mesh['head'=4,'z'=16,'core'=2,'hid'=4] {'hid'}, dimensions={0} | all-to-all | bytes 2097152 | tf_op jit(solution)/shard_map/all_to_all | solution.py:244
  131.8 2.8 %rescale.1.weights = bf16[3,512,256]{2,1,0:T(8,128)(2,1)} custom-call(s32[1]{0:T(128)} %bitcast.1.head_ref, f32[2]{0:T(128)} %head_rate.1, bf16[4,512,256]{2,1,0:T(8,128)(2,1)} %all_to_all.22.ortho, bf16[2,512,256]{2,1,0:T(8,128)(2,1)} %gate.5, bf16[2,512,256]{2,1,0:T(8,128)(2,1)} %up.5, bf16[2,256,512]{2,1,0:T(8,128)(2,1)} %down.5), custom_call_target="tpu_custom_call" | custom-call | flops 7864320 | bytes 2359296 | tf_op jit(solution)/shard_map/rescale/pallas_call | solution.py:188
  134.6 13.6 %collective-permute-start.1 = (bf16[3,512,256]{2,1,0:T(8,128)(2,1)}, bf16[3,512,256]{2,1,0:T(8,128)(2,1)S(1)}, u32[]{:S(2)}, u32[]{:S(2)}) collective-permute-start(bf16[3,512,256]{2,1,0:T(8,128)(2,1)} %rescale.1.weights), channel_id=1, source_target_pairs={{0,4},{4,0},{1,5},{5,1},{2,6},{6,2},{3,7},{7,3},{8,12},{12,8},{9,1... | collective-permute-start | bytes 2359304 | tf_op jit(solution)/shard_map/ppermute | solution.py:246
  148.3 2.9 %query.2.rest_0_ = bf16[4,512,256]{2,1,0:T(8,128)(2,1)} custom-call(s32[1]{0:T(128)} %bitcast.1.head_ref, bf16[512,1024]{1,0:T(8,128)(2,1)} %queries.3, bf16[3,512,256]{2,1,0:T(8,128)(2,1)} %rescale.1.weights), custom_call_target="tpu_custom_call" | custom-call | flops 402653184 | bytes 1048576 | tf_op jit(solution)/shard_map/query/pallas_call | solution.py:213
  151.2 0.0 collective-permute-done.1.weights
  151.2 0.0 copy-start
  151.2 0.9 copy-done
  152.1 2.9 %query.3 = bf16[4,512,256]{2,1,0:T(8,128)(2,1)} custom-call(s32[1]{0:T(128)} %bitcast.head_ref, bf16[512,1024]{1,0:T(8,128)(2,1)} %queries.3, bf16[3,512,256]{2,1,0:T(8,128)(2,1)} %copy-done, bf16[4,512,256]{2,1,0:T(8,128)(2,1)} %query.2.rest_0_), custom_call_target="tpu_custom_call", output_to_operand_aliasing={{}: (3, {})} | custom-call | flops 402653184 | bytes 1048576 | tf_op jit(solution)/shard_map/query/pallas_call | solution.py:213
  154.9 18.4 %all_to_all.23 = bf16[4,512,256]{2,1,0:T(8,128)(2,1)S(1)} all-to-all(bf16[4,512,256]{2,1,0:T(8,128)(2,1)} %query.3), channel_id=1, replica_groups=mesh['head'=4,'z'=16,'core'=2,'hid'=4] {'hid'}, dimensions={0} | all-to-all | bytes 2097152 | tf_op jit(solution)/shard_map/all_to_all | solution.py:24
  173.3 0.9 reduce_sum.25
  (1 shorter events, 0.0 us)
Async XLA Ops:
  5.4 12.8 %collective-permute-start = (bf16[16,3,32,256]{3,2,1,0:T(8,128)(2,1)}, bf16[16,3,32,256]{3,2,1,0:T(8,128)(2,1)S(1)}, u32[]{:S(2)}, u32[]{:S(2)}) collective-permute-start(bf16[16,3,32,256]{3,2,1,0:T(8,128)(2,1)} %gradients.3), channel_id=1, source_target_pairs={{0,4},{4,0},{1,5},{5,1},{2,6},{6,2},{3,7},{7,3},{8,12},{12,8},{9,1... | collective-permute-start | bytes 2359304 | tf_op jit(solution)/shard_map/ppermute | solution.py:237
  134.6 16.5 %collective-permute-start.1 = (bf16[3,512,256]{2,1,0:T(8,128)(2,1)}, bf16[3,512,256]{2,1,0:T(8,128)(2,1)S(1)}, u32[]{:S(2)}, u32[]{:S(2)}) collective-permute-start(bf16[3,512,256]{2,1,0:T(8,128)(2,1)} %rescale.1.weights), channel_id=1, source_target_pairs={{0,4},{4,0},{1,5},{5,1},{2,6},{6,2},{3,7},{7,3},{8,12},{12,8},{9,1... | collective-permute-start | bytes 2359304 | tf_op jit(solution)/shard_map/ppermute | solution.py:246
  151.2 0.9 copy-start

commit v5 on v4

v5 whole, which is shorter than its diff:
```python
import jax
import jax.numpy as jnp
from jax import lax
from jax.experimental import pallas as pl
from jax.experimental.pallas import tpu as pltpu
from jax.sharding import Mesh
from jax.sharding import PartitionSpec as P

NS_ITERS = 3
TOK = ("z", "core")
KINDS = 3
TILE = 128

poly_a = 3.4445
poly_b = -4.775
poly_c = 2.0315


def dot32(left, right, contract):
    return lax.dot_general(left, right, (contract, ((), ())), preferred_element_type=jnp.float32)


def sum_of_copies(pieces, axis):
    got = lax.all_to_all(pieces, axis, 0, 0, tiled=True)
    return jnp.sum(got.astype(jnp.float32), axis=0)


def sigmoid(value):
    return 1.0 / (1.0 + jnp.exp(-value))


def head_gradients(head, lines, values, rates, gate, up, down, out, target, d_gate, d_up, hidden):
    first = head == 0
    rows, width = lines.shape
    for start in range(0, rows, TILE):
        part = slice(start, start + TILE)
        rate = jnp.where(first, rates[0:1, part], rates[1:2, part])
        rate = jnp.broadcast_to(rate, (TILE, TILE)).T
        rate = jnp.concatenate([rate] * (width // TILE), axis=1)
        goal = (-(rate * values[part, :].astype(jnp.float32))).astype(jnp.bfloat16)
        target[part, :] = goal
        gate_pre = dot32(lines[part, :], gate[...], ((1,), (0,)))
        up_pre = dot32(lines[part, :], up[...], ((1,), (0,)))
        back = dot32(goal, down[...], ((1,), (1,)))
        gate_sig = sigmoid(gate_pre)
        active = gate_pre * gate_sig
        hidden[part, :] = (active * up_pre).astype(jnp.bfloat16)
        d_gate[part, :] = (back * up_pre * gate_sig * (1.0 + gate_pre * (1.0 - gate_sig))).astype(
            jnp.bfloat16
        )
        d_up[part, :] = (back * active).astype(jnp.bfloat16)
    depth, _, chunk, units = out.shape
    for kind, (left, right) in enumerate(((lines, d_gate), (lines, d_up), (target, hidden))):
        term = dot32(left[...], right[...], ((0,), (0,))).astype(jnp.bfloat16)
        out[:, kind] = term.reshape(depth, chunk, units)


def first_head_kernel(heads, rates, keys, values, gate, up, down, out, *rest):
    kept, held, work, sems = rest[:5], rest[5:10], rest[10:14], rest[14]
    width = held[0].shape[1]
    copies = []
    for turn, places in enumerate((held, kept)):
        head = heads[turn]
        columns = pl.ds(pl.multiple_of(head * width, width), width)
        sources = (keys.at[:, columns], values.at[:, columns], gate.at[head], up.at[head], down.at[head])
        for at, (source, place) in enumerate(zip(sources, places)):
            copy = pltpu.make_async_copy(source, place, sems.at[turn, at])
            copy.start()
            copies.append(copy)
    for copy in copies[:5]:
        copy.wait()
    lines, goals, own_gate, own_up, own_down = held
    head_gradients(heads[0], lines, goals, rates, own_gate, own_up, own_down, out, *work)
    for copy in copies[5:]:
        copy.wait()


def second_head_kernel(head_ref, rates, lines, values, gate, up, down, out, *work):
    head_gradients(head_ref[0], lines, values, rates, gate, up, down, out, *work)


def newton_schulz_kernel(blocks, out, iterate, product, gram, raw):
    count, rows, units = blocks.shape
    columns = [slice(at * units, (at + 1) * units) for at in range(count)]
    halves = [slice(at, at + units) for at in range(0, rows, units)]
    for at in range(count):
        iterate[:, columns[at]] = blocks[at]
    scale = None
    for iteration in range(NS_ITERS):
        if iteration == 0:
            trace = jnp.zeros((1, 1), jnp.float32)
            for half in halves:
                block = dot32(iterate[...], iterate[half, :], ((1,), (1,)))
                raw[:, half] = block
                square = block[half, :]
                line = lax.broadcasted_iota(jnp.int32, square.shape, 0)
                column = lax.broadcasted_iota(jnp.int32, square.shape, 1)
                trace = trace + jnp.sum(
                    jnp.where(line == column, square, 0.0), axis=(0, 1), keepdims=True
                )
            scale = 1.0 / (jnp.sqrt(trace) + 1e-07)
            for half in halves:
                gram[:, half] = (raw[:, half] * (scale * scale)).astype(jnp.bfloat16)
        else:
            for half in halves:
                gram[:, half] = dot32(iterate[...], iterate[half, :], ((1,), (1,))).astype(
                    jnp.bfloat16
                )
        for at in range(count):
            block = dot32(gram[...], iterate[:, columns[at]], ((1,), (0,)))
            if iteration == 0:
                block = block * scale
            product[:, columns[at]] = block.astype(jnp.bfloat16)
        for at in range(count):
            second = dot32(gram[...], product[:, columns[at]], ((1,), (0,)))
            leading = iterate[:, columns[at]].astype(jnp.float32)
            if iteration == 0:
                leading = leading * scale
            block = (
                poly_a * leading
                + poly_b * product[:, columns[at]].astype(jnp.float32)
                + poly_c * second
            ).astype(jnp.bfloat16)
            if iteration == NS_ITERS - 1:
                out[at] = block
            else:
                iterate[:, columns[at]] = block


def rescale_kernel(head_ref, head_rate, ortho, gate, up, down, out):
    step = head_rate[head_ref[0]]
    for kind in range(KINDS):
        if kind == 2:
            old = down[...].astype(jnp.float32).T
        else:
            old = (gate, up)[kind][...].astype(jnp.float32)
        fresh = old - step * ortho[kind].astype(jnp.float32)
        old_norm = jnp.sqrt(jnp.sum(old * old, axis=0, keepdims=True))
        new_norm = jnp.sqrt(jnp.sum(fresh * fresh, axis=0, keepdims=True) + 1e-06)
        out[kind] = (fresh * (old_norm / new_norm)).astype(jnp.bfloat16)


def query_kernel(head_ref, queries, weights, *rest):
    out = rest[-1]
    head = head_ref[0]
    _, width, units = weights.shape
    pieces = width // units
    rows = queries.shape[0]
    columns = pl.ds(pl.multiple_of(head * width, width), width)
    base = 0
    if len(rest) == 2:
        base = head * pieces
        out[pl.ds(pieces - base, pieces)] = rest[0][...]
    for start in range(0, rows, 2 * TILE):
        part = slice(start, start + 2 * TILE)
        lines = queries[part, columns]
        query_gate = dot32(lines, weights[0], ((1,), (0,)))
        query_up = dot32(lines, weights[1], ((1,), (0,)))
        query_hidden = (query_gate * sigmoid(query_gate) * query_up).astype(jnp.bfloat16)
        for at in range(pieces):
            features = weights[2, at * units : (at + 1) * units, :]
            out[base + at, part, :] = dot32(query_hidden, features, ((1,), (1,))).astype(
                jnp.bfloat16
            )


def cost(flops, operands):
    return pl.CostEstimate(flops=flops, transcendentals=0, bytes_accessed=operands)


def in_vmem(kernel, name, out_shape, scalars, operands, scratch, flops, far=()):
    near = pl.BlockSpec(memory_space=pltpu.VMEM)
    several = isinstance(out_shape, list)
    shapes = [jax.ShapeDtypeStruct(shape, jnp.bfloat16) for shape in (out_shape if several else [out_shape])]
    return pl.pallas_call(
        kernel,
        in_specs=[pl.BlockSpec(memory_space=pltpu.SMEM)] * len(scalars)
        + [near] * len(operands)
        + [pl.BlockSpec(memory_space=pltpu.HBM)] * len(far),
        out_specs=[near] * len(shapes) if several else near,
        out_shape=shapes if several else shapes[0],
        scratch_shapes=scratch,
        compiler_params=pltpu.CompilerParams(vmem_limit_bytes=20 * 2**20),
        cost_estimate=cost(flops, 2 * sum(operand.size for operand in (*operands, *far))),
        name=name,
    )(*scalars, *operands, *(pltpu.with_memory_space_constraint(each, pltpu.HBM) for each in far))


def buffer(*shape, dtype=jnp.bfloat16):
    return pltpu.VMEM(shape, dtype)


def first_gradients(heads, rates, keys, values, gate, up, down, depth):
    rows, width, units = keys.shape[0], *gate.shape[1:]
    held = [(rows, width), (rows, width), (width, units), (width, units), (units, width)]
    pieces = (depth, KINDS, width // depth, units)
    work = [buffer(rows, width)] + [buffer(rows, units)] * 3
    return in_vmem(
        first_head_kernel,
        "first_gradients",
        [pieces, *held],
        (heads,),
        (rates,),
        [buffer(*shape) for shape in held] + work + [pltpu.SemaphoreType.DMA((2, 5))],
        12 * rows * width * units,
        (keys, values, gate, up, down),
    )


def second_gradients(head, rates, lines, values, gate, up, down, depth):
    (rows, width), units = lines.shape, gate.shape[1]
    return in_vmem(
        second_head_kernel,
        "second_gradients",
        (depth, KINDS, width // depth, units),
        (head,),
        (rates, lines, values, gate, up, down),
        [buffer(rows, width)] + [buffer(rows, units)] * 3,
        12 * rows * width * units,
    )


def newton_schulz(blocks):
    count, rows, units = blocks.shape
    whole = buffer(rows, count * units)
    return in_vmem(
        newton_schulz_kernel,
        "newton_schulz",
        blocks.shape,
        (),
        (blocks,),
        [whole, whole, buffer(rows, rows), buffer(rows, rows, dtype=jnp.float32)],
        18 * rows * rows * count * units,
    )


def rescaled(head, head_rate, ortho, gate, up, down):
    width, units = gate.shape
    return in_vmem(
        rescale_kernel,
        "rescale",
        (KINDS, width, units),
        (head, head_rate),
        (ortho, gate, up, down),
        [],
        20 * KINDS * width * units,
    )


def query_terms(head, queries, weights, earlier=None):
    rows = queries.shape[0]
    _, width, units = weights.shape
    pieces = width // units
    return in_vmem(
        query_kernel,
        "query",
        (pieces if earlier is None else 2 * pieces, rows, units),
        (head,),
        (queries, weights) if earlier is None else (queries, weights, earlier),
        [],
        6 * rows * width * units,
    )


def local(queries, keys, values, token_rate, head_rate, w_gate, w_up, w_down):
    core = lax.axis_index("core").astype(jnp.int32)
    mine, theirs = core.reshape(1), (1 - core).reshape(1)
    swap = [(0, 1), (1, 0)]
    depth = lax.axis_size("z")
    rates = token_rate.T
    there, *held = first_gradients(
        jnp.stack((1 - core, core)), rates, keys, values, w_gate, w_up, w_down, depth
    )
    received = lax.ppermute(there, "core", swap)
    pieces = (
        second_gradients(mine, rates, *held, depth).astype(jnp.float32)
        + received.astype(jnp.float32)
    ).astype(jnp.bfloat16)
    owned = sum_of_copies(pieces, "z").astype(jnp.bfloat16)
    full = lax.all_gather(owned, "z", axis=1, tiled=True)
    blocks = lax.all_to_all(jnp.concatenate((full, full[:1]), axis=0), "hid", 0, 0, tiled=True)
    ortho = lax.all_to_all(newton_schulz(blocks), "hid", 0, 0, tiled=True)
    new = rescaled(mine, head_rate, ortho, *held[2:])
    new_there = lax.ppermute(new, "core", swap)
    terms = query_terms(theirs, queries, new_there, query_terms(mine, queries, new))
    return sum_of_copies(terms, "hid").astype(jnp.bfloat16)


def solution(mesh):
    finer = Mesh(
        mesh.devices.reshape(mesh.shape["head"], -1, 2, mesh.shape["hid"]),
        ("head", "z", "core", "hid"),
    )
    return jax.shard_map(
        local,
        mesh=finer,
        in_specs=(
            P(TOK, "head"),
            P(TOK, "head"),
            P(TOK, "head"),
            P(TOK, "head"),
            P("head"),
            P("head", None, "hid"),
            P("head", None, "hid"),
            P("head", "hid", None),
        ),
        out_specs=P(TOK, ("head", "hid")),
        check_vma=False,
    )
```

time: 175 us -> 159 us (0.909)
  Pallas kernels: 24.5 us -> 13.6 us
  blocking collectives: 122 us -> 118 us
  local copies, waits for them, and re-layouts: 2.48 us -> 0.72 us
    pallas_call x6, Pallas kernels: 24.5 us -> 13.6 us  [in_vmem(): pl.pallas_call(kernel, in_specs=[pl.BlockSpec(memory_space=pltpu.SMEM)] *...]
    all_to_all x2, blocking collectives: 64.9 us -> 62.4 us  [sum_of_copies(): got = lax.all_to_all(pieces, axis, 0, 0, tiled=True)]
    all_to_all x1, blocking collectives: 14.1 us -> 12.2 us  [local(): ortho = lax.all_to_all(newton_schulz(blocks), 'hid', 0, 0, tiled=True)]
    unnamed x3 -> x8, local copies, waits for them, and re-layouts: 2.46 us -> 0.7 us
  transfers between devices with their start and end apart: 2 -> 2, of which waited for: 0 -> 2; matrix products, arithmetic and copies ran while one was open for 0% -> 0% of each run, Pallas kernels for 4% -> 1%
where the time goes in v5:
time: 159 us; the launch traced here: 158 us
  blocking collectives  118 us (74%)
  starting transfers between devices  22.7 us (14%)
  Pallas kernels  13.6 us (9%)
    all_to_all x2, blocking collectives, sum_of_copies(): got = lax.all_to_all(pieces, axis, 0, 0, tiled=True)  62.4 us
    all_gather x1, blocking collectives, local(): full = lax.all_gather(owned, 'z', axis=1, tiled=True)  30.3 us
    ppermute x1, starting transfers between devices, local(): new_there = lax.ppermute(new, 'core', swap)  14 us
    pallas_call x6, Pallas kernels, in_vmem(): pl.pallas_call(kernel, in_specs=[pl.BlockSpec(memory_space=pltpu.SMEM)] *...  13.6 us
    all_to_all x1, blocking collectives, local(): lax.all_to_all(jnp.concatenate((full, full[:1]), axis=0), 'hid', 0, 0, ti...  13.6 us
    all_to_all x1, blocking collectives, local(): ortho = lax.all_to_all(newton_schulz(blocks), 'hid', 0, 0, tiled=True)  12.2 us
    ppermute x1, starting transfers between devices, local(): received = lax.ppermute(there, 'core', swap)  8.75 us
  transfers between devices with their start and end apart: 2, of which 2 were waited for; matrix products, arithmetic and copies ran while one was open for 0% of the time, Pallas kernels for 1%

profile of v5, /device:TPU:1, one launch (start us, length us, event | category | flops | bytes accessed | tf_op | source)
XLA Modules:
  0.0 158.5 jit_solution(12935132911526825666)
XLA Ops:
  0.0 0.1 pad_add_fusion.heads
  0.1 0.0 copy-start.1
  0.1 0.7 copy-done.1
  0.8 0.0 copy-start.2
  0.8 3.5 %first_gradients.1 = (bf16[16,3,32,256]{3,2,1,0:T(8,128)(2,1)S(1)}, bf16[512,512]{1,0:T(8,128)(2,1)S(1)}, bf16[512,512]{1,0:T(8,128)(2,1)S(1)}, bf16[512,256]{1,...) custom-call(s32[2]{0:T(128)S(1)} %pad_add_fusion.heads, f32[2,512]{1,0:T(2,128)S(1)} %bitcast.3, ...), custom_call_target="tpu_custom_call" | custom-call | flops 805306368 | bytes 3672064 | tf_op jit(solution)/shard_map/first_gradients/pallas_call | solution.py:175
  4.3 8.7 %collective-permute-start = (bf16[16,3,32,256]{3,2,1,0:T(8,128)(2,1)S(1)}, bf16[16,3,32,256]{3,2,1,0:T(8,128)(2,1)S(1)}, u32[]{:S(2)}, u32[]{:S(2)}) collective-permute-start(bf16[16,3,32,256]{3,2,1,0:T(8,128)(2,1)S(1)} %get-tuple-element.16), channel_id=1, source_target_pairs={{0,4},{4,0},{1,5},{5,1},{2,6},{6,2},{3,7},{7,3},{8,12},{12,8},{9,1... | collective-permute-start | bytes 2359304 | tf_op jit(solution)/shard_map/ppermute | solution.py:274
  13.0 0.0 copy-done.2
  13.1 1.5 second_gradients.1
  14.6 0.3 collective-permute-done
  14.9 0.3 add_convert_fusion
  15.3 45.1 %all_to_all.20 = bf16[16,3,32,256]{3,2,1,0:T(8,128)(2,1)S(1)} all-to-all(bf16[16,3,32,256]{3,2,1,0:T(8,128)(2,1)S(1)} %add_convert_fusion), channel_id=1, replica_groups=mesh['head'=4,'z'=16,'core'=2,'hid'=4] {'z'}, dimensions={0} | all-to-all | bytes 1572864 | tf_op jit(solution)/shard_map/all_to_all | solution.py:24
  60.4 0.1 reduce_sum.24
  60.5 30.3 %all_gather.3 = bf16[3,512,256]{2,1,0:T(8,128)(2,1)S(1)} all-gather(bf16[3,32,256]{2,1,0:T(8,128)(2,1)S(1)} %reduce_sum.24), channel_id=1, replica_groups=mesh['head'=4,'z'=16,'core'=2,'hid'=4] {'z'}, dimensions={1}, use_global_device_ids=true | all-gather | bytes 835584 | tf_op jit(solution)/shard_map/all_gather | solution.py:280
  90.8 0.1 pad_maximum_fusion
  90.9 13.6 %all_to_all.21.blocks = bf16[4,512,256]{2,1,0:T(8,128)(2,1)S(1)} all-to-all(bf16[4,512,256]{2,1,0:T(8,128)(2,1)S(1)} %pad_maximum_fusion), channel_id=1, replica_groups=mesh['head'=4,'z'=16,'core'=2,'hid'=4] {'hid'}, dimensions={0} | all-to-all | bytes 2097152 | tf_op jit(solution)/shard_map/all_to_all | solution.py:281
  104.5 5.9 %newton_schulz.1 = bf16[4,512,256]{2,1,0:T(8,128)(2,1)S(1)} custom-call(bf16[4,512,256]{2,1,0:T(8,128)(2,1)S(1)} %all_to_all.21.blocks), custom_call_target="tpu_custom_call" | custom-call | flops 4831838208 | bytes 1048576 | tf_op jit(solution)/shard_map/newton_schulz/pallas_call | solution.py:175
  110.4 0.0 copy-start.3
  110.4 12.2 %all_to_all.22.ortho = bf16[4,512,256]{2,1,0:T(8,128)(2,1)S(1)} all-to-all(bf16[4,512,256]{2,1,0:T(8,128)(2,1)S(1)} %newton_schulz.1), channel_id=1, replica_groups=mesh['head'=4,'z'=16,'core'=2,'hid'=4] {'hid'}, dimensions={0} | all-to-all | bytes 2097152 | tf_op jit(solution)/shard_map/all_to_all | solution.py:282
  122.6 0.0 copy-done.3
  122.6 0.0 copy-start
  122.6 1.1 rescale.1.weights
  123.7 14.0 %collective-permute-start.1 = (bf16[3,512,256]{2,1,0:T(8,128)(2,1)S(1)}, bf16[3,512,256]{2,1,0:T(8,128)(2,1)S(1)}, u32[]{:S(2)}, u32[]{:S(2)}) collective-permute-start(bf16[3,512,256]{2,1,0:T(8,128)(2,1)S(1)} %rescale.1.weights), channel_id=1, source_target_pairs={{0,4},{4,0},{1,5},{5,1},{2,6},{6,2},{3,7},{7,3},{8,12},{12,8},{9,1... | collective-permute-start | bytes 2359304 | tf_op jit(solution)/shard_map/ppermute | solution.py:284
  137.7 0.0 copy-done
  137.7 0.8 query.2.rest_0_
  138.5 1.1 collective-permute-done.1.weights
  139.6 0.8 query.3
  140.4 17.2 %all_to_all.23 = bf16[4,512,256]{2,1,0:T(8,128)(2,1)S(1)} all-to-all(bf16[4,512,256]{2,1,0:T(8,128)(2,1)S(1)} %query.3), channel_id=1, replica_groups=mesh['head'=4,'z'=16,'core'=2,'hid'=4] {'hid'}, dimensions={0} | all-to-all | bytes 2097152 | tf_op jit(solution)/shard_map/all_to_all | solution.py:24
  157.6 0.9 reduce_sum.25
  (1 shorter events, 0.0 us)
Async XLA Ops:
  0.1 0.7 copy-start.1
  0.8 12.3 %copy-start.2 = (f32[512,2]{0,1:T(2,128)S(1)}, f32[512,2]{0,1:T(2,128)}, u32[]{:S(2)}) copy-start(f32[512,2]{0,1:T(2,128)} %param.11) | copy-start | bytes 12292
  4.3 10.6 %collective-permute-start = (bf16[16,3,32,256]{3,2,1,0:T(8,128)(2,1)S(1)}, bf16[16,3,32,256]{3,2,1,0:T(8,128)(2,1)S(1)}, u32[]{:S(2)}, u32[]{:S(2)}) collective-permute-start(bf16[16,3,32,256]{3,2,1,0:T(8,128)(2,1)S(1)} %get-tuple-element.16), channel_id=1, source_target_pairs={{0,4},{4,0},{1,5},{5,1},{2,6},{6,2},{3,7},{7,3},{8,12},{12,8},{9,1... | collective-permute-start | bytes 2359304 | tf_op jit(solution)/shard_map/ppermute | solution.py:274
  110.4 12.2 %copy-start.3 = (f32[2]{0:T(128)S(1)}, f32[2]{0:T(128)}, u32[]{:S(2)}) copy-start(f32[2]{0:T(128)} %head_rate.1) | copy-start | bytes 28
  122.6 15.1 %copy-start = (bf16[512,1024]{1,0:T(8,128)(2,1)S(1)}, bf16[512,1024]{1,0:T(8,128)(2,1)}, u32[]{:S(2)}) copy-start(bf16[512,1024]{1,0:T(8,128)(2,1)} %queries.3) | copy-start | bytes 3145732
  123.7 15.9 %collective-permute-start.1 = (bf16[3,512,256]{2,1,0:T(8,128)(2,1)S(1)}, bf16[3,512,256]{2,1,0:T(8,128)(2,1)S(1)}, u32[]{:S(2)}, u32[]{:S(2)}) collective-permute-start(bf16[3,512,256]{2,1,0:T(8,128)(2,1)S(1)} %rescale.1.weights), channel_id=1, source_target_pairs={{0,4},{4,0},{1,5},{5,1},{2,6},{6,2},{3,7},{7,3},{8,12},{12,8},{9,1... | collective-permute-start | bytes 2359304 | tf_op jit(solution)/shard_map/ppermute | solution.py:284

commit v6 on v5

--- a/solution.py
+++ b/solution.py
@@ -7,7 +7,9 @@
 from jax.sharding import PartitionSpec as P
 
 NS_ITERS = 3
-TOK = ("z", "core")
+Z = ("far", "near")
+TOK = (*Z, "core")
+NEAR = 4
 KINDS = 3
 TILE = 128
 
@@ -55,10 +57,11 @@
         out[:, kind] = term.reshape(depth, chunk, units)
 
 
-def first_head_kernel(heads, rates, keys, values, gate, up, down, out, *rest):
-    kept, held, work, sems = rest[:5], rest[5:10], rest[10:14], rest[14]
+def first_head_kernel(heads, keys, values, gate, up, down, all_rates, out, *rest):
+    kept, rates, held, work, sems = rest[:5], rest[5], rest[6:11], rest[11:15], rest[15]
     width = held[0].shape[1]
-    copies = []
+    copies = [pltpu.make_async_copy(all_rates, rates, sems.at[2, 0])]
+    copies[0].start()
     for turn, places in enumerate((held, kept)):
         head = heads[turn]
         columns = pl.ds(pl.multiple_of(head * width, width), width)
@@ -67,11 +70,11 @@
             copy = pltpu.make_async_copy(source, place, sems.at[turn, at])
             copy.start()
             copies.append(copy)
-    for copy in copies[:5]:
+    for copy in copies[:6]:
         copy.wait()
     lines, goals, own_gate, own_up, own_down = held
     head_gradients(heads[0], lines, goals, rates, own_gate, own_up, own_down, out, *work)
-    for copy in copies[5:]:
+    for copy in copies[6:]:
         copy.wait()
 
 
@@ -79,13 +82,13 @@
     head_gradients(head_ref[0], lines, values, rates, gate, up, down, out, *work)
 
 
-def newton_schulz_kernel(blocks, out, iterate, product, gram, raw):
+def newton_schulz_kernel(blocks, out, iterate, gram, factor, raw):
     count, rows, units = blocks.shape
     columns = [slice(at * units, (at + 1) * units) for at in range(count)]
     halves = [slice(at, at + units) for at in range(0, rows, units)]
     for at in range(count):
         iterate[:, columns[at]] = blocks[at]
-    scale = None
+    scale = 1.0
     for iteration in range(NS_ITERS):
         if iteration == 0:
             trace = jnp.zeros((1, 1), jnp.float32)
@@ -106,25 +109,22 @@
                 gram[:, half] = dot32(iterate[...], iterate[half, :], ((1,), (1,))).astype(
                     jnp.bfloat16
                 )
+        for half in halves:
+            square = dot32(gram[...], gram[:, half], ((1,), (0,)))
+            factor[:, half] = (
+                poly_b * gram[:, half].astype(jnp.float32) + poly_c * square
+            ).astype(jnp.bfloat16)
         for at in range(count):
-            block = dot32(gram[...], iterate[:, columns[at]], ((1,), (0,)))
+            current = iterate[:, columns[at]]
+            block = poly_a * current.astype(jnp.float32) + dot32(
+                factor[...], current, ((1,), (0,))
+            )
             if iteration == 0:
                 block = block * scale
-            product[:, columns[at]] = block.astype(jnp.bfloat16)
-        for at in range(count):
-            second = dot32(gram[...], product[:, columns[at]], ((1,), (0,)))
-            leading = iterate[:, columns[at]].astype(jnp.float32)
-            if iteration == 0:
-                leading = leading * scale
-            block = (
-                poly_a * leading
-                + poly_b * product[:, columns[at]].astype(jnp.float32)
-                + poly_c * second
-            ).astype(jnp.bfloat16)
             if iteration == NS_ITERS - 1:
-                out[at] = block
+                out[at] = block.astype(jnp.bfloat16)
             else:
-                iterate[:, columns[at]] = block
+                iterate[:, columns[at]] = block.astype(jnp.bfloat16)
 
 
 def rescale_kernel(head_ref, head_rate, ortho, gate, up, down, out):
@@ -171,7 +171,10 @@
 def in_vmem(kernel, name, out_shape, scalars, operands, scratch, flops, far=()):
     near = pl.BlockSpec(memory_space=pltpu.VMEM)
     several = isinstance(out_shape, list)
-    shapes = [jax.ShapeDtypeStruct(shape, jnp.bfloat16) for shape in (out_shape if several else [out_shape])]
+    shapes = [
+        jax.ShapeDtypeStruct(shape, jnp.float32 if len(shape) == 2 and shape[0] == 2 else jnp.bfloat16)
+        for shape in (out_shape if several else [out_shape])
+    ]
     return pl.pallas_call(
         kernel,
         in_specs=[pl.BlockSpec(memory_space=pltpu.SMEM)] * len(scalars)
@@ -198,12 +201,12 @@
     return in_vmem(
         first_head_kernel,
         "first_gradients",
-        [pieces, *held],
+        [pieces, *held, rates.shape],
         (heads,),
-        (rates,),
-        [buffer(*shape) for shape in held] + work + [pltpu.SemaphoreType.DMA((2, 5))],
+        (),
+        [buffer(*shape) for shape in held] + work + [pltpu.SemaphoreType.DMA((3, 5))],
         12 * rows * width * units,
-        (keys, values, gate, up, down),
+        (keys, values, gate, up, down, rates),
     )
 
 
@@ -222,15 +225,19 @@
 
 def newton_schulz(blocks):
     count, rows, units = blocks.shape
-    whole = buffer(rows, count * units)
     return in_vmem(
         newton_schulz_kernel,
         "newton_schulz",
         blocks.shape,
         (),
         (blocks,),
-        [whole, whole, buffer(rows, rows), buffer(rows, rows, dtype=jnp.float32)],
-        18 * rows * rows * count * units,
+        [
+            buffer(rows, count * units),
+            buffer(rows, rows),
+            buffer(rows, rows),
+            buffer(rows, rows, dtype=jnp.float32),
+        ],
+        12 * rows * rows * count * units + 6 * rows**3,
     )
 
 
@@ -266,18 +273,19 @@
     core = lax.axis_index("core").astype(jnp.int32)
     mine, theirs = core.reshape(1), (1 - core).reshape(1)
     swap = [(0, 1), (1, 0)]
-    depth = lax.axis_size("z")
-    rates = token_rate.T
-    there, *held = first_gradients(
-        jnp.stack((1 - core, core)), rates, keys, values, w_gate, w_up, w_down, depth
+    near, far, depth = lax.axis_size("near"), lax.axis_size("far"), lax.axis_size(Z)
+    there, *held, rates = first_gradients(
+        jnp.stack((1 - core, core)), token_rate.T, keys, values, w_gate, w_up, w_down, depth
     )
     received = lax.ppermute(there, "core", swap)
     pieces = (
         second_gradients(mine, rates, *held, depth).astype(jnp.float32)
         + received.astype(jnp.float32)
     ).astype(jnp.bfloat16)
-    owned = sum_of_copies(pieces, "z").astype(jnp.bfloat16)
-    full = lax.all_gather(owned, "z", axis=1, tiled=True)
+    near_sum = sum_of_copies(pieces.reshape(near, far, *pieces.shape[1:]), "near")
+    owned = sum_of_copies(near_sum.astype(jnp.bfloat16), "far").astype(jnp.bfloat16)
+    full = lax.all_gather(owned, Z, axis=0).reshape(far, near, *owned.shape)
+    full = full.transpose(2, 1, 0, 3, 4).reshape(KINDS, -1, owned.shape[-1])
     blocks = lax.all_to_all(jnp.concatenate((full, full[:1]), axis=0), "hid", 0, 0, tiled=True)
     ortho = lax.all_to_all(newton_schulz(blocks), "hid", 0, 0, tiled=True)
     new = rescaled(mine, head_rate, ortho, *held[2:])
@@ -288,8 +296,8 @@
 
 def solution(mesh):
     finer = Mesh(
-        mesh.devices.reshape(mesh.shape["head"], -1, 2, mesh.shape["hid"]),
-        ("head", "z", "core", "hid"),
+        mesh.devices.reshape(mesh.shape["head"], -1, NEAR, 2, mesh.shape["hid"]),
+        ("head", *TOK, "hid"),
     )
     return jax.shard_map(
         local,

time: 159 us -> 155 us (0.975)
  blocking collectives: 118 us -> 115 us
  starting transfers between devices: 22.7 us -> 24.5 us
    all_gather x1, blocking collectives: 30.3 us -> 25.8 us  [local(): full = lax.all_gather(owned, Z, axis=0).reshape(far, near, *owned.shape)]
    ppermute x1, starting transfers between devices: 14 us -> 15.7 us  [local(): new_there = lax.ppermute(new, 'core', swap)]
    all_to_all x2 -> x3, blocking collectives: 62.4 us -> 62.4 us  [sum_of_copies(): got = lax.all_to_all(pieces, axis, 0, 0, tiled=True)]
where the time goes in v6:
time: 155 us
  blocking collectives  115 us (74%)
  starting transfers between devices  24.5 us (16%)
  Pallas kernels  12.5 us (8%)
  other arithmetic  1.56 us (1%)
    all_to_all x3, blocking collectives, sum_of_copies(): got = lax.all_to_all(pieces, axis, 0, 0, tiled=True)  62.4 us
    all_gather x1, blocking collectives, local(): full = lax.all_gather(owned, Z, axis=0).reshape(far, near, *owned.shape)  25.8 us
    ppermute x1, starting transfers between devices, local(): new_there = lax.ppermute(new, 'core', swap)  15.7 us
    all_to_all x1, blocking collectives, local(): lax.all_to_all(jnp.concatenate((full, full[:1]), axis=0), 'hid', 0, 0, ti...  13.6 us
    all_to_all x1, blocking collectives, local(): ortho = lax.all_to_all(newton_schulz(blocks), 'hid', 0, 0, tiled=True)  12.8 us
    pallas_call x6, Pallas kernels, in_vmem(): pl.pallas_call(kernel, in_specs=[pl.BlockSpec(memory_space=pltpu.SMEM)] *...  12.5 us
    ppermute x1, starting transfers between devices, local(): received = lax.ppermute(there, 'core', swap)  8.75 us
  transfers between devices with their start and end apart: 2, of which 2 were waited for; matrix products, arithmetic and copies ran while one was open for 0% of the time, Pallas kernels for 1%

profile of v6, /device:TPU:1, one launch (start us, length us, event | category | flops | bytes accessed | tf_op | source)
XLA Modules:
  0.0 154.8 jit_solution(15041658372920930136)
XLA Ops:
  0.0 0.1 pad_add_fusion.heads
  0.1 3.6 %first_gradients.1 = (bf16[16,3,32,256]{3,2,1,0:T(8,128)(2,1)S(1)}, bf16[512,512]{1,0:T(8,128)(2,1)S(1)}, bf16[512,512]{1,0:T(8,128)(2,1)S(1)}, bf16[512,256]{1,...) custom-call(s32[2]{0:T(128)S(1)} %pad_add_fusion.heads, ...), custom_call_target="tpu_custom_call" | custom-call | flops 805306368 | bytes 3672064 | tf_op jit(solution)/shard_map/first_gradients/pallas_call | solution.py:178
  3.7 8.7 %collective-permute-start = (bf16[16,3,32,256]{3,2,1,0:T(8,128)(2,1)S(1)}, bf16[16,3,32,256]{3,2,1,0:T(8,128)(2,1)S(1)}, u32[]{:S(2)}, u32[]{:S(2)}) collective-permute-start(bf16[16,3,32,256]{3,2,1,0:T(8,128)(2,1)S(1)} %get-tuple-element.18), channel_id=1, source_target_pairs={{0,4},{4,0},{1,5},{5,1},{2,6},{6,2},{3,7},{7,3},{8,12},{12,8},{9,1... | collective-permute-start | bytes 2359304 | tf_op jit(solution)/shard_map/ppermute | solution.py:280
  12.4 1.5 second_gradients.1
  13.9 0.4 collective-permute-done
  14.3 0.3 add_convert_fusion
  14.6 22.2 %all_to_all.25 = bf16[4,4,3,32,256]{4,3,2,1,0:T(8,128)(2,1)S(1)} all-to-all(bf16[4,4,3,32,256]{4,3,2,1,0:T(8,128)(2,1)S(1)} %bitcast.12), channel_id=1, replica_groups=mesh['head'=4,'far'=4,'near'=4,'core'=2,'hid'=4] {'near'}, dimensions={0} | all-to-all | bytes 1572864 | tf_op jit(solution)/shard_map/all_to_all | solution.py:26
  36.9 0.1 reduce_sum.36
  37.0 22.9 %all_to_all.26 = bf16[4,3,32,256]{3,2,1,0:T(8,128)(2,1)S(1)} all-to-all(bf16[4,3,32,256]{3,2,1,0:T(8,128)(2,1)S(1)} %reduce_sum.36), channel_id=1, replica_groups=mesh['head'=4,'far'=4,'near'=4,'core'=2,'hid'=4] {'far'}, dimensions={0} | all-to-all | bytes 393216 | tf_op jit(solution)/shard_map/all_to_all | solution.py:26
  59.9 25.8 %all-gather = bf16[48,32,256]{2,1,0:T(8,128)(2,1)S(1)} all-gather(bf16[3,32,256]{2,1,0:T(8,128)(2,1)S(1)} %reduce_sum.37), channel_id=2, replica_groups=mesh['head'=4,'far'=4,'near'=4,'core'=2,'hid'=4] {'far','near'}, dimensions={0}, use_global_device_ids=true | all-gather | bytes 835584 | tf_op jit(solution)/shard_map/all_gather | solution.py:287
  85.8 0.1 copy.13
  85.9 0.1 pad_maximum_fusion
  86.0 13.6 %all_to_all.27.blocks = bf16[4,512,256]{2,1,0:T(8,128)(2,1)S(1)} all-to-all(bf16[4,512,256]{2,1,0:T(8,128)(2,1)S(1)} %pad_maximum_fusion), channel_id=1, replica_groups=mesh['head'=4,'far'=4,'near'=4,'core'=2,'hid'=4] {'hid'}, dimensions={0} | all-to-all | bytes 2097152 | tf_op jit(solution)/shard_map/all_to_all | solution.py:289
  99.6 4.8 %newton_schulz.1 = bf16[4,512,256]{2,1,0:T(8,128)(2,1)S(1)} custom-call(bf16[4,512,256]{2,1,0:T(8,128)(2,1)S(1)} %all_to_all.27.blocks), custom_call_target="tpu_custom_call" | custom-call | flops 4026531840 | bytes 1048576 | tf_op jit(solution)/shard_map/newton_schulz/pallas_call | solution.py:178
  104.4 0.0 copy-start.1
  104.4 12.8 %all_to_all.28.ortho = bf16[4,512,256]{2,1,0:T(8,128)(2,1)S(1)} all-to-all(bf16[4,512,256]{2,1,0:T(8,128)(2,1)S(1)} %newton_schulz.1), channel_id=1, replica_groups=mesh['head'=4,'far'=4,'near'=4,'core'=2,'hid'=4] {'hid'}, dimensions={0} | all-to-all | bytes 2097152 | tf_op jit(solution)/shard_map/all_to_all | solution.py:290
  117.2 0.0 copy-done.1
  117.2 0.0 copy-start
  117.2 1.1 rescale.1.weights
  118.3 15.7 %collective-permute-start.1 = (bf16[3,512,256]{2,1,0:T(8,128)(2,1)S(1)}, bf16[3,512,256]{2,1,0:T(8,128)(2,1)S(1)}, u32[]{:S(2)}, u32[]{:S(2)}) collective-permute-start(bf16[3,512,256]{2,1,0:T(8,128)(2,1)S(1)} %rescale.1.weights), channel_id=1, source_target_pairs={{0,4},{4,0},{1,5},{5,1},{2,6},{6,2},{3,7},{7,3},{8,12},{12,8},{9,1... | collective-permute-start | bytes 2359304 | tf_op jit(solution)/shard_map/ppermute | solution.py:292
  134.0 0.0 copy-done
  134.0 0.8 query.2.rest_0_
  134.8 1.1 collective-permute-done.1.weights
  135.9 0.8 query.3
  136.7 17.2 %all_to_all.29 = bf16[4,512,256]{2,1,0:T(8,128)(2,1)S(1)} all-to-all(bf16[4,512,256]{2,1,0:T(8,128)(2,1)S(1)} %query.3), channel_id=1, replica_groups=mesh['head'=4,'far'=4,'near'=4,'core'=2,'hid'=4] {'hid'}, dimensions={0} | all-to-all | bytes 2097152 | tf_op jit(solution)/shard_map/all_to_all | solution.py:26
  153.9 0.9 reduce_sum.38
  (3 shorter events, 0.1 us)
Async XLA Ops:
  3.7 10.6 %collective-permute-start = (bf16[16,3,32,256]{3,2,1,0:T(8,128)(2,1)S(1)}, bf16[16,3,32,256]{3,2,1,0:T(8,128)(2,1)S(1)}, u32[]{:S(2)}, u32[]{:S(2)}) collective-permute-start(bf16[16,3,32,256]{3,2,1,0:T(8,128)(2,1)S(1)} %get-tuple-element.18), channel_id=1, source_target_pairs={{0,4},{4,0},{1,5},{5,1},{2,6},{6,2},{3,7},{7,3},{8,12},{12,8},{9,1... | collective-permute-start | bytes 2359304 | tf_op jit(solution)/shard_map/ppermute | solution.py:280
  104.4 12.8 %copy-start.1 = (f32[2]{0:T(128)S(1)}, f32[2]{0:T(128)}, u32[]{:S(2)}) copy-start(f32[2]{0:T(128)} %head_rate.1) | copy-start | bytes 28
  117.2 16.9 %copy-start = (bf16[512,1024]{1,0:T(8,128)(2,1)S(1)}, bf16[512,1024]{1,0:T(8,128)(2,1)}, u32[]{:S(2)}) copy-start(bf16[512,1024]{1,0:T(8,128)(2,1)} %queries.3) | copy-start | bytes 3145732
  118.3 17.6 %collective-permute-start.1 = (bf16[3,512,256]{2,1,0:T(8,128)(2,1)S(1)}, bf16[3,512,256]{2,1,0:T(8,128)(2,1)S(1)}, u32[]{:S(2)}, u32[]{:S(2)}) collective-permute-start(bf16[3,512,256]{2,1,0:T(8,128)(2,1)S(1)} %rescale.1.weights), channel_id=1, source_target_pairs={{0,4},{4,0},{1,5},{5,1},{2,6},{6,2},{3,7},{7,3},{8,12},{12,8},{9,1... | collective-permute-start | bytes 2359304 | tf_op jit(solution)/shard_map/ppermute | solution.py:292

commit v7 on v6

--- a/solution.py
+++ b/solution.py
@@ -7,8 +7,7 @@
 from jax.sharding import PartitionSpec as P
 
 NS_ITERS = 3
-Z = ("far", "near")
-TOK = (*Z, "core")
+TOK = ("far", "near", "core")
 NEAR = 4
 KINDS = 3
 TILE = 128
@@ -273,7 +272,7 @@
     core = lax.axis_index("core").astype(jnp.int32)
     mine, theirs = core.reshape(1), (1 - core).reshape(1)
     swap = [(0, 1), (1, 0)]
-    near, far, depth = lax.axis_size("near"), lax.axis_size("far"), lax.axis_size(Z)
+    depth = lax.axis_size("near")
     there, *held, rates = first_gradients(
         jnp.stack((1 - core, core)), token_rate.T, keys, values, w_gate, w_up, w_down, depth
     )
@@ -282,10 +281,11 @@
         second_gradients(mine, rates, *held, depth).astype(jnp.float32)
         + received.astype(jnp.float32)
     ).astype(jnp.bfloat16)
-    near_sum = sum_of_copies(pieces.reshape(near, far, *pieces.shape[1:]), "near")
-    owned = sum_of_copies(near_sum.astype(jnp.bfloat16), "far").astype(jnp.bfloat16)
-    full = lax.all_gather(owned, Z, axis=0).reshape(far, near, *owned.shape)
-    full = full.transpose(2, 1, 0, 3, 4).reshape(KINDS, -1, owned.shape[-1])
+    near_sum = sum_of_copies(pieces, "near").astype(jnp.bfloat16)
+    partials = lax.all_gather(near_sum, "far", axis=0)
+    owned = jnp.sum(partials.astype(jnp.float32), axis=0).astype(jnp.bfloat16)
+    full = lax.all_gather(owned, "near", axis=0)
+    full = full.transpose(1, 0, 2, 3).reshape(KINDS, -1, owned.shape[-1])
     blocks = lax.all_to_all(jnp.concatenate((full, full[:1]), axis=0), "hid", 0, 0, tiled=True)
     ortho = lax.all_to_all(newton_schulz(blocks), "hid", 0, 0, tiled=True)
     new = rescaled(mine, head_rate, ortho, *held[2:])

time: 155 us -> 153 us (0.987)
  starting transfers between devices: 24.5 us -> 16.2 us
  blocking collectives: 115 us -> 120 us
    all_gather x1 -> x2, blocking collectives: 25.8 us -> 52.8 us  [the longest x1 37.2 us: local(): partials = lax.all_gather(near_sum, 'far', axis=0)]
    all_to_all x3 -> x2, blocking collectives: 62.4 us -> 39.5 us  [sum_of_copies(): got = lax.all_to_all(pieces, axis, 0, 0, tiled=True)]
    ppermute x1, starting transfers between devices: 15.7 us -> 7.41 us  [local(): new_there = lax.ppermute(new, 'core', swap)]
    all_to_all x1, blocking collectives: 13.6 us -> 15.2 us  [local(): lax.all_to_all(jnp.concatenate((full, full[:1]), axis=0), 'hid', 0, 0, ti...]
where the time goes in v7:
time: 153 us; the launch traced here: 152 us
  blocking collectives  120 us (78%)
  starting transfers between devices  16.2 us (11%)
  Pallas kernels  12.5 us (8%)
  other arithmetic  1.64 us (1%)
    all_to_all x2, blocking collectives, sum_of_copies(): got = lax.all_to_all(pieces, axis, 0, 0, tiled=True)  39.5 us
    all_gather x1, blocking collectives, local(): partials = lax.all_gather(near_sum, 'far', axis=0)  37.2 us
    all_gather x1, blocking collectives, local(): full = lax.all_gather(owned, 'near', axis=0)  15.6 us
    all_to_all x1, blocking collectives, local(): lax.all_to_all(jnp.concatenate((full, full[:1]), axis=0), 'hid', 0, 0, ti...  15.2 us
    all_to_all x1, blocking collectives, local(): ortho = lax.all_to_all(newton_schulz(blocks), 'hid', 0, 0, tiled=True)  13 us
    pallas_call x6, Pallas kernels, in_vmem(): pl.pallas_call(kernel, in_specs=[pl.BlockSpec(memory_space=pltpu.SMEM)] *...  12.5 us
    ppermute x1, starting transfers between devices, local(): received = lax.ppermute(there, 'core', swap)  8.75 us
    ppermute x1, starting transfers between devices, local(): new_there = lax.ppermute(new, 'core', swap)  7.41 us
  transfers between devices with their start and end apart: 2, of which 2 were waited for; matrix products, arithmetic and copies ran while one was open for 0% of the time, Pallas kernels for 1%

profile of v7, /device:TPU:1, one launch (start us, length us, event | category | flops | bytes accessed | tf_op | source)
XLA Modules:
  0.0 152.5 jit_solution(2114077241306684408)
XLA Ops:
  0.0 0.1 pad_add_fusion.heads
  0.1 3.6 %first_gradients.1 = (bf16[4,3,128,256]{3,2,1,0:T(8,128)(2,1)S(1)}, bf16[512,512]{1,0:T(8,128)(2,1)S(1)}, bf16[512,512]{1,0:T(8,128)(2,1)S(1)}, bf16[512,256]{1,...) custom-call(s32[2]{0:T(128)S(1)} %pad_add_fusion.heads, ...), custom_call_target="tpu_custom_call" | custom-call | flops 805306368 | bytes 3672064 | tf_op jit(solution)/shard_map/first_gradients/pallas_call | solution.py:177
  3.7 8.7 %collective-permute-start = (bf16[4,3,128,256]{3,2,1,0:T(8,128)(2,1)S(1)}, bf16[4,3,128,256]{3,2,1,0:T(8,128)(2,1)S(1)}, u32[]{:S(2)}, u32[]{:S(2)}) collective-permute-start(bf16[4,3,128,256]{3,2,1,0:T(8,128)(2,1)S(1)} %get-tuple-element.18), channel_id=1, source_target_pairs={{0,4},{4,0},{1,5},{5,1},{2,6},{6,2},{3,7},{7,3},{8,12},{12,8},{9,1... | collective-permute-start | bytes 2359304 | tf_op jit(solution)/shard_map/ppermute | solution.py:279
  12.4 1.5 second_gradients.1
  13.9 0.4 collective-permute-done
  14.3 0.2 add_convert_fusion
  14.5 22.2 %all_to_all.20 = bf16[4,3,128,256]{3,2,1,0:T(8,128)(2,1)S(1)} all-to-all(bf16[4,3,128,256]{3,2,1,0:T(8,128)(2,1)S(1)} %add_convert_fusion), channel_id=1, replica_groups=mesh['head'=4,'far'=4,'near'=4,'core'=2,'hid'=4] {'near'}, dimensions={0} | all-to-all | bytes 1572864 | tf_op jit(solution)/shard_map/all_to_all | solution.py:25
  36.8 0.2 reduce_sum.36
  37.0 37.2 %all-gather = bf16[12,128,256]{2,1,0:T(8,128)(2,1)S(1)} all-gather(bf16[3,128,256]{2,1,0:T(8,128)(2,1)S(1)} %reduce_sum.36), channel_id=2, replica_groups=mesh['head'=4,'far'=4,'near'=4,'core'=2,'hid'=4] {'far'}, dimensions={0}, use_global_device_ids=true | all-gather | bytes 983040 | tf_op jit(solution)/shard_map/all_gather | solution.py:285
  74.1 0.2 reduce_sum.37
  74.3 15.6 %all-gather.1 = bf16[12,128,256]{2,1,0:T(8,128)(2,1)S(1)} all-gather(bf16[3,128,256]{2,1,0:T(8,128)(2,1)S(1)} %reduce_sum.37), channel_id=3, replica_groups=mesh['head'=4,'far'=4,'near'=4,'core'=2,'hid'=4] {'near'}, dimensions={0}, use_global_device_ids=true | all-gather | bytes 983040 | tf_op jit(solution)/shard_map/all_gather | solution.py:287
  89.9 0.1 copy.10
  90.0 0.1 pad_maximum_fusion
  90.1 15.2 %all_to_all.21.blocks = bf16[4,512,256]{2,1,0:T(8,128)(2,1)S(1)} all-to-all(bf16[4,512,256]{2,1,0:T(8,128)(2,1)S(1)} %pad_maximum_fusion), channel_id=1, replica_groups=mesh['head'=4,'far'=4,'near'=4,'core'=2,'hid'=4] {'hid'}, dimensions={0} | all-to-all | bytes 2097152 | tf_op jit(solution)/shard_map/all_to_all | solution.py:289
  105.3 4.8 %newton_schulz.1 = bf16[4,512,256]{2,1,0:T(8,128)(2,1)S(1)} custom-call(bf16[4,512,256]{2,1,0:T(8,128)(2,1)S(1)} %all_to_all.21.blocks), custom_call_target="tpu_custom_call" | custom-call | flops 4026531840 | bytes 1048576 | tf_op jit(solution)/shard_map/newton_schulz/pallas_call | solution.py:177
  110.1 0.0 copy-start.1
  110.1 13.0 %all_to_all.22.ortho = bf16[4,512,256]{2,1,0:T(8,128)(2,1)S(1)} all-to-all(bf16[4,512,256]{2,1,0:T(8,128)(2,1)S(1)} %newton_schulz.1), channel_id=1, replica_groups=mesh['head'=4,'far'=4,'near'=4,'core'=2,'hid'=4] {'hid'}, dimensions={0} | all-to-all | bytes 2097152 | tf_op jit(solution)/shard_map/all_to_all | solution.py:290
  123.1 0.0 copy-done.1
  123.1 0.0 copy-start
  123.1 1.1 rescale.1.weights
  124.2 7.4 %collective-permute-start.1 = (bf16[3,512,256]{2,1,0:T(8,128)(2,1)S(1)}, bf16[3,512,256]{2,1,0:T(8,128)(2,1)S(1)}, u32[]{:S(2)}, u32[]{:S(2)}) collective-permute-start(bf16[3,512,256]{2,1,0:T(8,128)(2,1)S(1)} %rescale.1.weights), channel_id=1, source_target_pairs={{0,4},{4,0},{1,5},{5,1},{2,6},{6,2},{3,7},{7,3},{8,12},{12,8},{9,1... | collective-permute-start | bytes 2359304 | tf_op jit(solution)/shard_map/ppermute | solution.py:292
  131.7 0.0 copy-done
  131.7 0.8 query.2.rest_0_
  132.4 1.1 collective-permute-done.1.weights
  133.5 0.8 query.3
  134.3 17.2 %all_to_all.23 = bf16[4,512,256]{2,1,0:T(8,128)(2,1)S(1)} all-to-all(bf16[4,512,256]{2,1,0:T(8,128)(2,1)S(1)} %query.3), channel_id=1, replica_groups=mesh['head'=4,'far'=4,'near'=4,'core'=2,'hid'=4] {'hid'}, dimensions={0} | all-to-all | bytes 2097152 | tf_op jit(solution)/shard_map/all_to_all | solution.py:25
  151.6 0.9 reduce_sum.38
  (1 shorter events, 0.0 us)
Async XLA Ops:
  3.7 10.6 %collective-permute-start = (bf16[4,3,128,256]{3,2,1,0:T(8,128)(2,1)S(1)}, bf16[4,3,128,256]{3,2,1,0:T(8,128)(2,1)S(1)}, u32[]{:S(2)}, u32[]{:S(2)}) collective-permute-start(bf16[4,3,128,256]{3,2,1,0:T(8,128)(2,1)S(1)} %get-tuple-element.18), channel_id=1, source_target_pairs={{0,4},{4,0},{1,5},{5,1},{2,6},{6,2},{3,7},{7,3},{8,12},{12,8},{9,1... | collective-permute-start | bytes 2359304 | tf_op jit(solution)/shard_map/ppermute | solution.py:279
  110.1 13.0 %copy-start.1 = (f32[2]{0:T(128)S(1)}, f32[2]{0:T(128)}, u32[]{:S(2)}) copy-start(f32[2]{0:T(128)} %head_rate.1) | copy-start | bytes 28
  123.1 8.5 %copy-start = (bf16[512,1024]{1,0:T(8,128)(2,1)S(1)}, bf16[512,1024]{1,0:T(8,128)(2,1)}, u32[]{:S(2)}) copy-start(bf16[512,1024]{1,0:T(8,128)(2,1)} %queries.3) | copy-start | bytes 3145732
  124.2 9.3 %collective-permute-start.1 = (bf16[3,512,256]{2,1,0:T(8,128)(2,1)S(1)}, bf16[3,512,256]{2,1,0:T(8,128)(2,1)S(1)}, u32[]{:S(2)}, u32[]{:S(2)}) collective-permute-start(bf16[3,512,256]{2,1,0:T(8,128)(2,1)S(1)} %rescale.1.weights), channel_id=1, source_target_pairs={{0,4},{4,0},{1,5},{5,1},{2,6},{6,2},{3,7},{7,3},{8,12},{12,8},{9,1... | collective-permute-start | bytes 2359304 | tf_op jit(solution)/shard_map/ppermute | solution.py:292

commit v8 on v7

--- a/solution.py
+++ b/solution.py
@@ -30,11 +30,15 @@
     return 1.0 / (1.0 + jnp.exp(-value))
 
 
-def head_gradients(head, lines, values, rates, gate, up, down, out, target, d_gate, d_up, hidden):
+def head_gradients(
+    head, lines, values, rates, gate, up, down, out, target, d_gate, d_up, hidden, before=None
+):
     first = head == 0
     rows, width = lines.shape
     for start in range(0, rows, TILE):
         part = slice(start, start + TILE)
+        if before is not None:
+            before(start // TILE)
         rate = jnp.where(first, rates[0:1, part], rates[1:2, part])
         rate = jnp.broadcast_to(rate, (TILE, TILE)).T
         rate = jnp.concatenate([rate] * (width // TILE), axis=1)
@@ -58,23 +62,45 @@
 
 def first_head_kernel(heads, keys, values, gate, up, down, all_rates, out, *rest):
     kept, rates, held, work, sems = rest[:5], rest[5], rest[6:11], rest[11:15], rest[15]
-    width = held[0].shape[1]
-    copies = [pltpu.make_async_copy(all_rates, rates, sems.at[2, 0])]
-    copies[0].start()
-    for turn, places in enumerate((held, kept)):
-        head = heads[turn]
-        columns = pl.ds(pl.multiple_of(head * width, width), width)
-        sources = (keys.at[:, columns], values.at[:, columns], gate.at[head], up.at[head], down.at[head])
-        for at, (source, place) in enumerate(zip(sources, places)):
-            copy = pltpu.make_async_copy(source, place, sems.at[turn, at])
-            copy.start()
-            copies.append(copy)
-    for copy in copies[:6]:
-        copy.wait()
+    rows, width = held[0].shape
+    parts = [pl.ds(start, min(TILE, rows)) for start in range(0, rows, TILE)]
+
+    def sources(turn):
+        columns = pl.ds(pl.multiple_of(heads[turn] * width, width), width)
+        return columns, [each.at[heads[turn]] for each in (gate, up, down)]
+
+    columns, weights = sources(0)
+    loads = list(zip((all_rates, *weights), (rates, *held[2:])))
+    for part in parts:
+        for whole, place in zip((keys, values), held):
+            loads.append((whole.at[part, columns], place.at[part, :]))
+    loads = [
+        pltpu.make_async_copy(source, place, sems.at[0, at])
+        for at, (source, place) in enumerate(loads)
+    ]
+    columns, weights = sources(1)
+    later = [
+        pltpu.make_async_copy(source, place, sems.at[1, at])
+        for at, (source, place) in enumerate(
+            zip((keys.at[:, columns], values.at[:, columns], *weights), kept)
+        )
+    ]
+    for load in loads:
+        load.start()
+
+    def before(step):
+        for load in loads[:6] if step == 0 else loads[4 + 2 * step : 6 + 2 * step]:
+            load.wait()
+        if step == 0:
+            for load in later:
+                load.start()
+
     lines, goals, own_gate, own_up, own_down = held
-    head_gradients(heads[0], lines, goals, rates, own_gate, own_up, own_down, out, *work)
-    for copy in copies[6:]:
-        copy.wait()
+    head_gradients(
+        heads[0], lines, goals, rates, own_gate, own_up, own_down, out, *work, before=before
+    )
+    for load in later:
+        load.wait()
 
 
 def second_head_kernel(head_ref, rates, lines, values, gate, up, down, out, *work):
@@ -203,7 +229,7 @@
         [pieces, *held, rates.shape],
         (heads,),
         (),
-        [buffer(*shape) for shape in held] + work + [pltpu.SemaphoreType.DMA((3, 5))],
+        [buffer(*shape) for shape in held] + work + [pltpu.SemaphoreType.DMA((2, 4 + 2 * pl.cdiv(rows, TILE)))],
         12 * rows * width * units,
         (keys, values, gate, up, down, rates),
     )
@@ -284,8 +310,7 @@
     near_sum = sum_of_copies(pieces, "near").astype(jnp.bfloat16)
     partials = lax.all_gather(near_sum, "far", axis=0)
     owned = jnp.sum(partials.astype(jnp.float32), axis=0).astype(jnp.bfloat16)
-    full = lax.all_gather(owned, "near", axis=0)
-    full = full.transpose(1, 0, 2, 3).reshape(KINDS, -1, owned.shape[-1])
+    full = lax.all_gather(owned, "near", axis=1, tiled=True)
     blocks = lax.all_to_all(jnp.concatenate((full, full[:1]), axis=0), "hid", 0, 0, tiled=True)
     ortho = lax.all_to_all(newton_schulz(blocks), "hid", 0, 0, tiled=True)
     new = rescaled(mine, head_rate, ortho, *held[2:])

time: 153 us -> 154 us (level)
  no operation moved by 1% of the time
where the time goes in v8:
time: 154 us; the launch traced here: 153 us
  blocking collectives  120 us (78%)
  starting transfers between devices  16.2 us (11%)
  Pallas kernels  12.7 us (8%)
  other arithmetic  1.64 us (1%)
    all_to_all x2, blocking collectives, sum_of_copies(): got = lax.all_to_all(pieces, axis, 0, 0, tiled=True)  39.5 us
    all_gather x1, blocking collectives, local(): partials = lax.all_gather(near_sum, 'far', axis=0)  37.4 us
    all_gather x1, blocking collectives, local(): full = lax.all_gather(owned, 'near', axis=1, tiled=True)  16 us
    all_to_all x1, blocking collectives, local(): lax.all_to_all(jnp.concatenate((full, full[:1]), axis=0), 'hid', 0, 0, ti...  14.6 us
    all_to_all x1, blocking collectives, local(): ortho = lax.all_to_all(newton_schulz(blocks), 'hid', 0, 0, tiled=True)  13 us
    pallas_call x6, Pallas kernels, in_vmem(): pl.pallas_call(kernel, in_specs=[pl.BlockSpec(memory_space=pltpu.SMEM)] *...  12.7 us
    ppermute x1, starting transfers between devices, local(): received = lax.ppermute(there, 'core', swap)  8.75 us
    ppermute x1, starting transfers between devices, local(): new_there = lax.ppermute(new, 'core', swap)  7.41 us
  transfers between devices with their start and end apart: 2, of which 2 were waited for; matrix products, arithmetic and copies ran while one was open for 0% of the time, Pallas kernels for 1%

profile of v8, /device:TPU:1, one launch (start us, length us, event | category | flops | bytes accessed | tf_op | source)
XLA Modules:
  0.0 152.6 jit_solution(12955733029254087273)
XLA Ops:
  0.0 0.1 pad_add_fusion.heads
  0.1 3.8 %first_gradients.1 = (bf16[4,3,128,256]{3,2,1,0:T(8,128)(2,1)S(1)}, bf16[512,512]{1,0:T(8,128)(2,1)S(1)}, bf16[512,512]{1,0:T(8,128)(2,1)S(1)}, bf16[512,256]{1,...) custom-call(s32[2]{0:T(128)S(1)} %pad_add_fusion.heads, ...), custom_call_target="tpu_custom_call" | custom-call | flops 805306368 | bytes 3672064 | tf_op jit(solution)/shard_map/first_gradients/pallas_call | solution.py:203
  3.9 8.7 %collective-permute-start = (bf16[4,3,128,256]{3,2,1,0:T(8,128)(2,1)S(1)}, bf16[4,3,128,256]{3,2,1,0:T(8,128)(2,1)S(1)}, u32[]{:S(2)}, u32[]{:S(2)}) collective-permute-start(bf16[4,3,128,256]{3,2,1,0:T(8,128)(2,1)S(1)} %get-tuple-element.18), channel_id=1, source_target_pairs={{0,4},{4,0},{1,5},{5,1},{2,6},{6,2},{3,7},{7,3},{8,12},{12,8},{9,1... | collective-permute-start | bytes 2359304 | tf_op jit(solution)/shard_map/ppermute | solution.py:305
  12.6 1.5 second_gradients.1
  14.1 0.4 collective-permute-done
  14.5 0.2 add_convert_fusion
  14.8 22.2 %all_to_all.20 = bf16[4,3,128,256]{3,2,1,0:T(8,128)(2,1)S(1)} all-to-all(bf16[4,3,128,256]{3,2,1,0:T(8,128)(2,1)S(1)} %add_convert_fusion), channel_id=1, replica_groups=mesh['head'=4,'far'=4,'near'=4,'core'=2,'hid'=4] {'near'}, dimensions={0} | all-to-all | bytes 1572864 | tf_op jit(solution)/shard_map/all_to_all | solution.py:25
  37.0 0.2 reduce_sum.36
  37.2 37.4 %all-gather = bf16[12,128,256]{2,1,0:T(8,128)(2,1)S(1)} all-gather(bf16[3,128,256]{2,1,0:T(8,128)(2,1)S(1)} %reduce_sum.36), channel_id=2, replica_groups=mesh['head'=4,'far'=4,'near'=4,'core'=2,'hid'=4] {'far'}, dimensions={0}, use_global_device_ids=true | all-gather | bytes 983040 | tf_op jit(solution)/shard_map/all_gather | solution.py:311
  74.6 0.2 reduce_sum.37
  74.7 16.0 %all_gather.11 = bf16[3,512,256]{2,1,0:T(8,128)(2,1)S(1)} all-gather(bf16[3,128,256]{2,1,0:T(8,128)(2,1)S(1)} %reduce_sum.37), channel_id=1, replica_groups=mesh['head'=4,'far'=4,'near'=4,'core'=2,'hid'=4] {'near'}, dimensions={1}, use_global_device_ids=true | all-gather | bytes 983040 | tf_op jit(solution)/shard_map/all_gather | solution.py:313
  90.8 0.1 pad_maximum_fusion
  90.9 14.6 %all_to_all.21.blocks = bf16[4,512,256]{2,1,0:T(8,128)(2,1)S(1)} all-to-all(bf16[4,512,256]{2,1,0:T(8,128)(2,1)S(1)} %pad_maximum_fusion), channel_id=1, replica_groups=mesh['head'=4,'far'=4,'near'=4,'core'=2,'hid'=4] {'hid'}, dimensions={0} | all-to-all | bytes 2097152 | tf_op jit(solution)/shard_map/all_to_all | solution.py:314
  105.5 4.8 %newton_schulz.1 = bf16[4,512,256]{2,1,0:T(8,128)(2,1)S(1)} custom-call(bf16[4,512,256]{2,1,0:T(8,128)(2,1)S(1)} %all_to_all.21.blocks), custom_call_target="tpu_custom_call" | custom-call | flops 4026531840 | bytes 1048576 | tf_op jit(solution)/shard_map/newton_schulz/pallas_call | solution.py:203
  110.3 0.0 copy-start.1
  110.3 13.0 %all_to_all.22.ortho = bf16[4,512,256]{2,1,0:T(8,128)(2,1)S(1)} all-to-all(bf16[4,512,256]{2,1,0:T(8,128)(2,1)S(1)} %newton_schulz.1), channel_id=1, replica_groups=mesh['head'=4,'far'=4,'near'=4,'core'=2,'hid'=4] {'hid'}, dimensions={0} | all-to-all | bytes 2097152 | tf_op jit(solution)/shard_map/all_to_all | solution.py:315
  123.3 0.0 copy-done.1
  123.3 0.0 copy-start
  123.3 1.1 rescale.1.weights
  124.4 7.4 %collective-permute-start.1 = (bf16[3,512,256]{2,1,0:T(8,128)(2,1)S(1)}, bf16[3,512,256]{2,1,0:T(8,128)(2,1)S(1)}, u32[]{:S(2)}, u32[]{:S(2)}) collective-permute-start(bf16[3,512,256]{2,1,0:T(8,128)(2,1)S(1)} %rescale.1.weights), channel_id=1, source_target_pairs={{0,4},{4,0},{1,5},{5,1},{2,6},{6,2},{3,7},{7,3},{8,12},{12,8},{9,1... | collective-permute-start | bytes 2359304 | tf_op jit(solution)/shard_map/ppermute | solution.py:317
  131.8 0.0 copy-done
  131.8 0.8 query.2.rest_0_
  132.6 1.1 collective-permute-done.1.weights
  133.7 0.8 query.3
  134.5 17.2 %all_to_all.23 = bf16[4,512,256]{2,1,0:T(8,128)(2,1)S(1)} all-to-all(bf16[4,512,256]{2,1,0:T(8,128)(2,1)S(1)} %query.3), channel_id=1, replica_groups=mesh['head'=4,'far'=4,'near'=4,'core'=2,'hid'=4] {'hid'}, dimensions={0} | all-to-all | bytes 2097152 | tf_op jit(solution)/shard_map/all_to_all | solution.py:25
  151.7 0.9 reduce_sum.38
  (1 shorter events, 0.0 us)
Async XLA Ops:
  3.9 10.6 %collective-permute-start = (bf16[4,3,128,256]{3,2,1,0:T(8,128)(2,1)S(1)}, bf16[4,3,128,256]{3,2,1,0:T(8,128)(2,1)S(1)}, u32[]{:S(2)}, u32[]{:S(2)}) collective-permute-start(bf16[4,3,128,256]{3,2,1,0:T(8,128)(2,1)S(1)} %get-tuple-element.18), channel_id=1, source_target_pairs={{0,4},{4,0},{1,5},{5,1},{2,6},{6,2},{3,7},{7,3},{8,12},{12,8},{9,1... | collective-permute-start | bytes 2359304 | tf_op jit(solution)/shard_map/ppermute | solution.py:305
  110.3 13.0 %copy-start.1 = (f32[2]{0:T(128)S(1)}, f32[2]{0:T(128)}, u32[]{:S(2)}) copy-start(f32[2]{0:T(128)} %head_rate.1) | copy-start | bytes 28
  123.3 8.5 %copy-start = (bf16[512,1024]{1,0:T(8,128)(2,1)S(1)}, bf16[512,1024]{1,0:T(8,128)(2,1)}, u32[]{:S(2)}) copy-start(bf16[512,1024]{1,0:T(8,128)(2,1)} %queries.3) | copy-start | bytes 3145732
  124.4 9.3 %collective-permute-start.1 = (bf16[3,512,256]{2,1,0:T(8,128)(2,1)S(1)}, bf16[3,512,256]{2,1,0:T(8,128)(2,1)S(1)}, u32[]{:S(2)}, u32[]{:S(2)}) collective-permute-start(bf16[3,512,256]{2,1,0:T(8,128)(2,1)S(1)} %rescale.1.weights), channel_id=1, source_target_pairs={{0,4},{4,0},{1,5},{5,1},{2,6},{6,2},{3,7},{7,3},{8,12},{12,8},{9,1... | collective-permute-start | bytes 2359304 | tf_op jit(solution)/shard_map/ppermute | solution.py:317

commit v9 on v7

--- a/solution.py
+++ b/solution.py
@@ -67,10 +67,13 @@
         sources = (keys.at[:, columns], values.at[:, columns], gate.at[head], up.at[head], down.at[head])
         for at, (source, place) in enumerate(zip(sources, places)):
             copy = pltpu.make_async_copy(source, place, sems.at[turn, at])
-            copy.start()
+            if turn == 0:
+                copy.start()
             copies.append(copy)
     for copy in copies[:6]:
         copy.wait()
+    for copy in copies[6:]:
+        copy.start()
     lines, goals, own_gate, own_up, own_down = held
     head_gradients(heads[0], lines, goals, rates, own_gate, own_up, own_down, out, *work)
     for copy in copies[6:]:
@@ -284,8 +287,7 @@
     near_sum = sum_of_copies(pieces, "near").astype(jnp.bfloat16)
     partials = lax.all_gather(near_sum, "far", axis=0)
     owned = jnp.sum(partials.astype(jnp.float32), axis=0).astype(jnp.bfloat16)
-    full = lax.all_gather(owned, "near", axis=0)
-    full = full.transpose(1, 0, 2, 3).reshape(KINDS, -1, owned.shape[-1])
+    full = lax.all_gather(owned, "near", axis=1, tiled=True)
     blocks = lax.all_to_all(jnp.concatenate((full, full[:1]), axis=0), "hid", 0, 0, tiled=True)
     ortho = lax.all_to_all(newton_schulz(blocks), "hid", 0, 0, tiled=True)
     new = rescaled(mine, head_rate, ortho, *held[2:])

time: 153 us -> 154 us (level)
  blocking collectives: 120 us -> 122 us
where the time goes in v9:
time: 154 us
  blocking collectives  122 us (79%)
  starting transfers between devices  15.6 us (10%)
  Pallas kernels  12.6 us (8%)
  other arithmetic  1.64 us (1%)
    all_to_all x2, blocking collectives, sum_of_copies(): got = lax.all_to_all(pieces, axis, 0, 0, tiled=True)  39.5 us
    all_gather x1, blocking collectives, local(): partials = lax.all_gather(near_sum, 'far', axis=0)  37.2 us
    all_to_all x1, blocking collectives, local(): lax.all_to_all(jnp.concatenate((full, full[:1]), axis=0), 'hid', 0, 0, ti...  16.4 us
    all_gather x1, blocking collectives, local(): full = lax.all_gather(owned, 'near', axis=1, tiled=True)  15.6 us
    all_to_all x1, blocking collectives, local(): ortho = lax.all_to_all(newton_schulz(blocks), 'hid', 0, 0, tiled=True)  13.6 us
    pallas_call x6, Pallas kernels, in_vmem(): pl.pallas_call(kernel, in_specs=[pl.BlockSpec(memory_space=pltpu.SMEM)] *...  12.6 us
    ppermute x1, starting transfers between devices, local(): received = lax.ppermute(there, 'core', swap)  8.75 us
    ppermute x1, starting transfers between devices, local(): new_there = lax.ppermute(new, 'core', swap)  6.81 us
  transfers between devices with their start and end apart: 2, of which 2 were waited for; matrix products, arithmetic and copies ran while one was open for 0% of the time, Pallas kernels for 1%

profile of v9, /device:TPU:1, one launch (start us, length us, event | category | flops | bytes accessed | tf_op | source)
XLA Modules:
  0.0 153.7 jit_solution(2825051167121403571)
XLA Ops:
  0.0 0.1 pad_add_fusion.heads
  0.1 3.7 %first_gradients.1 = (bf16[4,3,128,256]{3,2,1,0:T(8,128)(2,1)S(1)}, bf16[512,512]{1,0:T(8,128)(2,1)S(1)}, bf16[512,512]{1,0:T(8,128)(2,1)S(1)}, bf16[512,256]{1,...) custom-call(s32[2]{0:T(128)S(1)} %pad_add_fusion.heads, ...), custom_call_target="tpu_custom_call" | custom-call | flops 805306368 | bytes 3672064 | tf_op jit(solution)/shard_map/first_gradients/pallas_call | solution.py:180
  3.8 8.7 %collective-permute-start = (bf16[4,3,128,256]{3,2,1,0:T(8,128)(2,1)S(1)}, bf16[4,3,128,256]{3,2,1,0:T(8,128)(2,1)S(1)}, u32[]{:S(2)}, u32[]{:S(2)}) collective-permute-start(bf16[4,3,128,256]{3,2,1,0:T(8,128)(2,1)S(1)} %get-tuple-element.18), channel_id=1, source_target_pairs={{0,4},{4,0},{1,5},{5,1},{2,6},{6,2},{3,7},{7,3},{8,12},{12,8},{9,1... | collective-permute-start | bytes 2359304 | tf_op jit(solution)/shard_map/ppermute | solution.py:282
  12.5 1.5 second_gradients.1
  14.0 0.4 collective-permute-done
  14.4 0.2 add_convert_fusion
  14.7 22.2 %all_to_all.20 = bf16[4,3,128,256]{3,2,1,0:T(8,128)(2,1)S(1)} all-to-all(bf16[4,3,128,256]{3,2,1,0:T(8,128)(2,1)S(1)} %add_convert_fusion), channel_id=1, replica_groups=mesh['head'=4,'far'=4,'near'=4,'core'=2,'hid'=4] {'near'}, dimensions={0} | all-to-all | bytes 1572864 | tf_op jit(solution)/shard_map/all_to_all | solution.py:25
  36.9 0.2 reduce_sum.36
  37.1 37.2 %all-gather = bf16[12,128,256]{2,1,0:T(8,128)(2,1)S(1)} all-gather(bf16[3,128,256]{2,1,0:T(8,128)(2,1)S(1)} %reduce_sum.36), channel_id=2, replica_groups=mesh['head'=4,'far'=4,'near'=4,'core'=2,'hid'=4] {'far'}, dimensions={0}, use_global_device_ids=true | all-gather | bytes 983040 | tf_op jit(solution)/shard_map/all_gather | solution.py:288
  74.2 0.2 reduce_sum.37
  74.4 15.6 %all_gather.11 = bf16[3,512,256]{2,1,0:T(8,128)(2,1)S(1)} all-gather(bf16[3,128,256]{2,1,0:T(8,128)(2,1)S(1)} %reduce_sum.37), channel_id=1, replica_groups=mesh['head'=4,'far'=4,'near'=4,'core'=2,'hid'=4] {'near'}, dimensions={1}, use_global_device_ids=true | all-gather | bytes 983040 | tf_op jit(solution)/shard_map/all_gather | solution.py:290
  90.1 0.1 pad_maximum_fusion
  90.2 16.4 %all_to_all.21.blocks = bf16[4,512,256]{2,1,0:T(8,128)(2,1)S(1)} all-to-all(bf16[4,512,256]{2,1,0:T(8,128)(2,1)S(1)} %pad_maximum_fusion), channel_id=1, replica_groups=mesh['head'=4,'far'=4,'near'=4,'core'=2,'hid'=4] {'hid'}, dimensions={0} | all-to-all | bytes 2097152 | tf_op jit(solution)/shard_map/all_to_all | solution.py:291
  106.5 4.8 %newton_schulz.1 = bf16[4,512,256]{2,1,0:T(8,128)(2,1)S(1)} custom-call(bf16[4,512,256]{2,1,0:T(8,128)(2,1)S(1)} %all_to_all.21.blocks), custom_call_target="tpu_custom_call" | custom-call | flops 4026531840 | bytes 1048576 | tf_op jit(solution)/shard_map/newton_schulz/pallas_call | solution.py:180
  111.3 0.0 copy-start.1
  111.4 13.6 %all_to_all.22.ortho = bf16[4,512,256]{2,1,0:T(8,128)(2,1)S(1)} all-to-all(bf16[4,512,256]{2,1,0:T(8,128)(2,1)S(1)} %newton_schulz.1), channel_id=1, replica_groups=mesh['head'=4,'far'=4,'near'=4,'core'=2,'hid'=4] {'hid'}, dimensions={0} | all-to-all | bytes 2097152 | tf_op jit(solution)/shard_map/all_to_all | solution.py:292
  124.9 0.0 copy-done.1
  124.9 0.0 copy-start
  124.9 1.1 rescale.1.weights
  126.0 6.8 %collective-permute-start.1 = (bf16[3,512,256]{2,1,0:T(8,128)(2,1)S(1)}, bf16[3,512,256]{2,1,0:T(8,128)(2,1)S(1)}, u32[]{:S(2)}, u32[]{:S(2)}) collective-permute-start(bf16[3,512,256]{2,1,0:T(8,128)(2,1)S(1)} %rescale.1.weights), channel_id=1, source_target_pairs={{0,4},{4,0},{1,5},{5,1},{2,6},{6,2},{3,7},{7,3},{8,12},{12,8},{9,1... | collective-permute-start | bytes 2359304 | tf_op jit(solution)/shard_map/ppermute | solution.py:294
  132.9 0.0 copy-done
  132.9 0.8 query.2.rest_0_
  133.7 1.1 collective-permute-done.1.weights
  134.8 0.8 query.3
  135.5 17.2 %all_to_all.23 = bf16[4,512,256]{2,1,0:T(8,128)(2,1)S(1)} all-to-all(bf16[4,512,256]{2,1,0:T(8,128)(2,1)S(1)} %query.3), channel_id=1, replica_groups=mesh['head'=4,'far'=4,'near'=4,'core'=2,'hid'=4] {'hid'}, dimensions={0} | all-to-all | bytes 2097152 | tf_op jit(solution)/shard_map/all_to_all | solution.py:25
  152.8 0.9 reduce_sum.38
  (1 shorter events, 0.0 us)
Async XLA Ops:
  3.8 10.6 %collective-permute-start = (bf16[4,3,128,256]{3,2,1,0:T(8,128)(2,1)S(1)}, bf16[4,3,128,256]{3,2,1,0:T(8,128)(2,1)S(1)}, u32[]{:S(2)}, u32[]{:S(2)}) collective-permute-start(bf16[4,3,128,256]{3,2,1,0:T(8,128)(2,1)S(1)} %get-tuple-element.18), channel_id=1, source_target_pairs={{0,4},{4,0},{1,5},{5,1},{2,6},{6,2},{3,7},{7,3},{8,12},{12,8},{9,1... | collective-permute-start | bytes 2359304 | tf_op jit(solution)/shard_map/ppermute | solution.py:282
  111.3 13.6 %copy-start.1 = (f32[2]{0:T(128)S(1)}, f32[2]{0:T(128)}, u32[]{:S(2)}) copy-start(f32[2]{0:T(128)} %head_rate.1) | copy-start | bytes 28
  124.9 7.9 %copy-start = (bf16[512,1024]{1,0:T(8,128)(2,1)S(1)}, bf16[512,1024]{1,0:T(8,128)(2,1)}, u32[]{:S(2)}) copy-start(bf16[512,1024]{1,0:T(8,128)(2,1)} %queries.3) | copy-start | bytes 3145732
  126.0 8.7 %collective-permute-start.1 = (bf16[3,512,256]{2,1,0:T(8,128)(2,1)S(1)}, bf16[3,512,256]{2,1,0:T(8,128)(2,1)S(1)}, u32[]{:S(2)}, u32[]{:S(2)}) collective-permute-start(bf16[3,512,256]{2,1,0:T(8,128)(2,1)S(1)} %rescale.1.weights), channel_id=1, source_target_pairs={{0,4},{4,0},{1,5},{5,1},{2,6},{6,2},{3,7},{7,3},{8,12},{12,8},{9,1... | collective-permute-start | bytes 2359304 | tf_op jit(solution)/shard_map/ppermute | solution.py:294
